TPU v7x, 512 devices: a whole 4x4x16 slice. The times are simulated.
512 devices in a mesh: dp: 32 (over z, y_lo), pipe: 8 (over x, core), tensor: 2 (over y_hi).
Axes of the slice: x: 4, y: 4 (y_hi: 2, y_lo: 2; y = y_hi * 2 + y_lo), z: 16, core: 2. Of those that a mesh axis runs over, the one named last changes fastest.
Arguments:
- hidden: bfloat16 [8, 4096, 3584], P('pipe', 'dp', 'tensor'), may hold values from -6 to 6
- frozen_weight: bfloat16 [3584, 3584], P('dp', 'tensor'), may hold values from -1 to 1
- final_norm_gain: float32 [3584], P('tensor'), may hold values from 0.1 to 1.9
- adapter_down_maps: bfloat16 [8, 32, 3584], P(None, None, 'tensor'), may hold values from -0.09375 to 0.09375
- adapter_up_maps: bfloat16 [8, 32, 3584], P(None, None, 'tensor'), may hold values from -1 to 1
- tenant: int32 [8, 256], P('pipe'), may hold values from 0 to 7, as said below
- adapter: int32 [8], P('pipe'), may hold values from 0 to 7
Outputs:
- upstream_grad: bfloat16 [8, 4096, 3584], P('pipe', 'dp', 'tensor')
- grad_up: float32 [8, 32, 3584], P('pipe', None, 'tensor')
- grad_down: float32 [8, 32, 3584], P('pipe', None, 'tensor')
- row_loss: float32 [8, 256], P('pipe', 'dp')
Inputs may be any that keep to these rules, and one draw needn't show every extreme that they name: Rows 2i and 2i + 1 of a micro-batch have the same tenant.
All inputs are finite; a program needn't handle non-finite values.
Results may differ from a plain program's by a relative error of at most 0.024.
Values may be sent and summed in bfloat16 or wider, within the bound.
A program may use at most 64 MiB of HBM per device.

v0:
```python
import jax
import jax.numpy as jnp
from jax import lax
from jax.sharding import Mesh
from jax.sharding import PartitionSpec as P

MODEL_WIDTH = 3584
SEQ = 16
DP = ("dp_0", "dp_1")


logit_divisor = 0.05
loss_scale = 256.0
adapter_scale = 0.5
epsilon = 1e-06


def sent_to_all(array, axis):
    peers = lax.axis_size(axis)
    return lax.all_to_all(
        jnp.broadcast_to(array[None], (peers, *array.shape)), axis, 0, 0, tiled=True
    )


def laid_out(parts, dim):
    parts = jnp.moveaxis(parts, 0, dim)
    shape = parts.shape
    return parts.reshape(*shape[:dim], shape[dim] * shape[dim + 1], *shape[dim + 2 :])


def gathered_copies(array, axis, dim):
    parts = sent_to_all(array, axis)
    return laid_out(parts, dim)


def whole_of(array, axes, dim):
    whole = array
    for number in range(len(axes) - 1, -1, -1):
        whole = lax.all_gather(whole, axes[number], axis=dim, tiled=True)
    return whole


def over_copies(array, axis):
    everything = sent_to_all(array, axis)
    return jnp.sum(everything, axis=0)


def packed_total(arrays, axis):
    flat, at, outs = (jnp.concatenate([a.reshape(-1) for a in arrays]), 0, [])
    subtotal = over_copies(flat, axis)
    for a in arrays:
        outs.append(subtotal[at : at + a.size].reshape(a.shape))
        at += a.size
    return tuple(outs)


def split_up(array, dim, peers):
    before, after = (array.shape[:dim], array.shape[dim + 1 :])
    return jnp.moveaxis(array.reshape(*before, peers, -1, *after), dim, 0)


def sum_at_owner(array, axis, dim):
    peers = lax.axis_size(axis)
    parts = lax.all_to_all(split_up(array, dim, peers), axis, 0, 0, tiled=True)
    return jnp.sum(parts.astype(jnp.float32), axis=0)


def passed_along(block, axis, distance):
    devices = range(lax.axis_size(axis))
    route = [((i - distance) % len(devices), i) for i in devices]
    return lax.ppermute(block, axis, route)


def filled_up(lines, peers):
    spare = -lines.shape[0] % peers
    if not spare:
        return lines
    return jnp.concatenate([lines, jnp.zeros((spare, *lines.shape[1:]), lines.dtype)])


def nested_sum(array, axes):
    lines = array.reshape(-1, array.shape[-1])
    own = sum_at_owner(filled_up(lines, lax.axis_size(axes)), axes, 0)
    whole = gathered_copies(own.astype(jnp.bfloat16), axes, 0)
    return whole[: len(lines)].reshape(array.shape).astype(jnp.float32)


def body(
    hidden, frozen_weight, final_norm_gain, adapter_down_maps, adapter_up_maps, tenant, adapter
):
    own_tokens = hidden[0]
    token_count = own_tokens.shape[0]
    half_width = own_tokens.shape[1]
    rows_local = token_count // SEQ
    full_tokens = gathered_copies(own_tokens, "tensor", 1)
    picked_adapter = adapter[0]
    down_matrix = lax.dynamic_index_in_dim(adapter_down_maps, picked_adapter, 0, keepdims=False)
    up_matrix = lax.dynamic_index_in_dim(adapter_up_maps, picked_adapter, 0, keepdims=False)
    low_part = lax.dot_general(
        own_tokens, down_matrix, (((1,), (1,)), ((), ())), preferred_element_type=jnp.float32
    )
    full_weight = whole_of(frozen_weight, DP, 0)
    frozen_output = jnp.dot(full_tokens, full_weight, preferred_element_type=jnp.float32)
    low_rank_hidden = over_copies(low_part, "tensor").astype(jnp.bfloat16)
    output_rows = frozen_output + adapter_scale * jnp.dot(
        low_rank_hidden, up_matrix, preferred_element_type=jnp.float32
    )
    token_squares = over_copies(jnp.sum(output_rows * output_rows, axis=1), "tensor")
    token_inv = lax.rsqrt(token_squares / MODEL_WIDTH + epsilon)
    gained = output_rows * final_norm_gain[None, :]
    normed = gained * token_inv[:, None]
    pooled = jnp.mean(normed.reshape(rows_local, SEQ, half_width), axis=1)
    squares = over_copies(jnp.sum(pooled * pooled, axis=1), "tensor")
    inverse = lax.rsqrt(squares + epsilon)
    unit_rows = pooled * inverse[:, None]
    encoded_vectors = unit_rows.astype(jnp.bfloat16)
    all_rows = whole_of(encoded_vectors, DP, 0)
    total_rows = all_rows.shape[0]
    logit_blocks = lax.dot_general(
        encoded_vectors, all_rows, (((1,), (1,)), ((), ())), preferred_element_type=jnp.float32
    )
    cosine_logits = over_copies(logit_blocks, "tensor") / logit_divisor
    position = lax.axis_index(DP)
    own_ids = position * rows_local + jnp.arange(rows_local, dtype=jnp.int32)
    every_id = jnp.arange(total_rows, dtype=jnp.int32)
    tenants_all = tenant[0]
    own_tenants = lax.dynamic_slice_in_dim(tenants_all, position * rows_local, rows_local)
    allowed = (own_tenants[:, None] == tenants_all[None, :]) & (
        own_ids[:, None] != every_id[None, :]
    )
    partner = every_id[None, :] == (own_ids ^ 1)[:, None]
    partner_float = partner.astype(jnp.float32)
    exps = jnp.where(allowed, jnp.exp(cosine_logits), 0.0)
    log_total = jnp.log(jnp.sum(exps, axis=1))
    positive = jnp.sum(jnp.where(partner, cosine_logits, 0.0), axis=1)
    row_loss = log_total - positive
    probs = jnp.where(allowed, jnp.exp(cosine_logits - log_total[:, None]), 0.0)
    weights = (loss_scale * (probs - partner_float)).astype(jnp.bfloat16)
    matching_logits = jnp.dot(weights, all_rows, preferred_element_type=jnp.float32)
    all_totals = gathered_copies(log_total, DP, 0)
    column_probs = jnp.where(allowed, jnp.exp(cosine_logits - all_totals[None, :]), 0.0)
    column_weights = (loss_scale * (column_probs - partner_float)).astype(jnp.bfloat16)
    groups = lax.axis_size(DP)
    grouped_weights = column_weights.reshape(rows_local, groups, rows_local)
    grouped_rows = all_rows.reshape(groups, rows_local, half_width)
    far_terms = jnp.einsum(
        "jki,kid->kjd", grouped_weights, grouped_rows, preferred_element_type=jnp.float32
    ).astype(jnp.bfloat16)
    far_terms = lax.optimization_barrier(far_terms)
    distractor_logits = jnp.sum(far_terms.astype(jnp.float32), axis=0)
    encoded_vector_derivative = (matching_logits + distractor_logits) / logit_divisor
    gained_rows = gained.reshape(rows_local, SEQ, half_width)
    along_part = jnp.sum(unit_rows * encoded_vector_derivative, axis=1)
    first_part = jnp.einsum("rsd,rd->rs", gained_rows, encoded_vector_derivative)
    second_part = jnp.einsum("rsd,rd->rs", gained_rows, unit_rows)
    along, first_sum, second_sum = packed_total((along_part, first_part, second_part), "tensor")
    grad_pool = inverse[:, None] * (encoded_vector_derivative - unit_rows * along[:, None])
    inner = (inverse[:, None] * (first_sum - along[:, None] * second_sum) / SEQ).reshape(
        token_count
    )
    spread = jnp.broadcast_to(
        (grad_pool * final_norm_gain[None, :])[:, None, :] / SEQ, (rows_local, SEQ, half_width)
    ).reshape(token_count, half_width)
    grad_norm_in = token_inv[:, None] * (
        spread - output_rows * (inner * token_inv * token_inv / MODEL_WIDTH)[:, None]
    )
    output_gradient = grad_norm_in.astype(jnp.bfloat16)
    low_rank_grad_piece = adapter_scale * lax.dot_general(
        output_gradient, up_matrix, (((1,), (1,)), ((), ())), preferred_element_type=jnp.float32
    )
    low_rank_gradient = over_copies(low_rank_grad_piece, "tensor").astype(jnp.bfloat16)
    base_terms = lax.dot_general(
        output_gradient, full_weight, (((1,), (1,)), ((), ())), preferred_element_type=jnp.float32
    )
    base_sum = sum_at_owner(base_terms.astype(jnp.bfloat16), "tensor", 1)
    grad_in = (
        base_sum + jnp.dot(low_rank_gradient, down_matrix, preferred_element_type=jnp.float32)
    ).astype(jnp.bfloat16)
    handed = passed_along(grad_in, "pipe", -1)
    up_map_piece = adapter_scale * lax.dot_general(
        low_rank_hidden,
        output_gradient,
        (((0,), (0,)), ((), ())),
        preferred_element_type=jnp.float32,
    )
    downward_part = lax.dot_general(
        low_rank_gradient, own_tokens, (((0,), (0,)), ((), ())), preferred_element_type=jnp.float32
    )
    up_map_gradient, grad_downward = (
        nested_sum(up_map_piece.astype(jnp.bfloat16), DP),
        nested_sum(downward_part.astype(jnp.bfloat16), DP),
    )
    return (handed[None], up_map_gradient[None], grad_downward[None], row_loss[None])


def solution(mesh):
    finer = Mesh(
        mesh.devices.reshape(16, 2, mesh.shape["pipe"], mesh.shape["tensor"]),
        ("dp_0", "dp_1", "pipe", "tensor"),
    )
    placed = (
        P("pipe", DP, "tensor"),
        P(DP, "tensor"),
        P("tensor"),
        P(None, None, "tensor"),
        P(None, None, "tensor"),
        P("pipe", None),
        P("pipe"),
    )
    return jax.shard_map(
        body,
        mesh=finer,
        in_specs=placed,
        out_specs=(
            P("pipe", DP, "tensor"),
            P("pipe", None, "tensor"),
            P("pipe", None, "tensor"),
            P("pipe", DP),
        ),
        check_vma=False,
    )
```

profile of v0, /device:TPU:2, one launch (start us, length us, event | category | flops | bytes accessed | tf_op | source)
XLA Modules:
  0.0 397.8 jit_solution(1148383375876992637)
XLA Ops:
  7.2 13.7 %all_gather.12 = bf16[224,1792]{1,0:T(8,128)(2,1)} all-gather(bf16[112,1792]{1,0:T(8,128)(2,1)} %param.8), channel_id=1, replica_groups=mesh['dp_0'=16,'dp_1'=2,'pipe'=8,'tensor'=2] {'dp_1'}, dimensions={0}, use_global_device_ids=true | all-gather | bytes 1204224 | tf_op jit(solution)/shard_map/all_gather | solution.py:39
  21.6 1.3 convolution_bitcast_fusion
  22.9 0.7 broadcast_in_dim.37
  23.6 4.2 %all-to-all-start.1 = ((f32[2,128,32]{1,2,0:T(8,128)}), f32[2,128,32]{1,2,0:T(8,128)S(1)}, u32[]{:S(2)}, u32[]{:S(2)}) async-start(f32[2,128,32]{1,2,0:T(8,128)} %broadcast_in_dim.37), calls=%async_computation.1 | async-start | bytes 65536 | tf_op jit(solution)/shard_map/all_to_all | solution.py:20
  27.7 1.3 copy.48
  29.0 4.2 %all-to-all-done.1 = f32[2,128,32]{1,2,0:T(8,128)S(1)} async-done(((f32[2,128,32]{1,2,0:T(8,128)}), f32[2,128,32]{1,2,0:T(8,128)S(1)}, u32[]{:S(2)}, u32[]{:S(2)}) %all-to-all-start.1) | async-done | bytes 32800 | tf_op jit(solution)/shard_map/all_to_all | solution.py:20
  33.2 1.1 broadcast_in_dim.36
  34.3 3.7 all-to-all-start
  38.0 11.9 %all-to-all-done = bf16[2,128,1792]{1,2,0:T(8,128)(2,1)S(1)} async-done(((bf16[2,128,1792]{1,2,0:T(8,128)(2,1)}), bf16[2,128,1792]{1,2,0:T(8,128)(2,1)S(1)}, u32[]{:S(2)}, u32[]{:S(2)}) %all-to-all-start) | async-done | bytes 917536 | tf_op jit(solution)/shard_map/all_to_all | solution.py:20
  49.9 126.0 %all-gather.2.cloned.1.call-done = bf16[3584,1792]{1,0:T(8,128)(2,1)} async-done(((bf16[224,1792]{1,0:T(8,128)(2,1)}), bf16[3584,1792]{1,0:T(8,128)(2,1)}) %all-gather.2.cloned.1.call-update) | async-done | bytes 12845072 | tf_op jit(solution)/shard_map/all_gather | solution.py:39
  175.9 6.6 %fusion.43 = f32[128,1792]{1,0:T(8,128)S(1)} fusion(bf16[128,3584]{0,1:T(8,128)(2,1)S(1)} %bitcast.87, bf16[3584,1792]{1,0:T(8,128)(2,1)} %all-gather.2.cloned.1.call-done), kind=kOutput, calls=%fused_computation.84 | convolution fusion | flops 1644167168 | bytes 14680064 | tf_op jit(solution)/shard_map/dot_general | solution.py:103
  182.5 0.4 multiply_reduce_fusion
  182.9 0.6 broadcast_in_dim.38
  183.4 4.3 %all-to-all-start.2 = ((f32[2,1,128]{2,1,0:T(1,128)}), f32[2,1,128]{2,1,0:T(1,128)S(1)}, u32[]{:S(2)}, u32[]{:S(2)}) async-start(f32[2,1,128]{2,1,0:T(1,128)} %broadcast_in_dim.38), calls=%async_computation.2 | async-start | bytes 2048 | tf_op jit(solution)/shard_map/all_to_all | solution.py:20
  187.8 0.5 broadcast.127
  188.3 0.7 reduce.10
  189.1 3.8 all-to-all-done.2
  193.0 0.3 bitcast_reduce_fusion
  193.4 7.6 %all_to_all.69 = f32[2,1,8]{2,1,0:T(1,128)S(1)} all-to-all(f32[2,1,8]{2,1,0:T(1,128)S(1)} %broadcast_in_dim.39), channel_id=1, replica_groups=mesh['dp_0'=16,'dp_1'=2,'pipe'=8,'tensor'=2] {'tensor'}, dimensions={0} | all-to-all | bytes 128 | tf_op jit(solution)/shard_map/all_to_all | solution.py:20
  201.1 4.5 %all_gather.14 = bf16[16,1792]{1,0:T(8,128)(2,1)S(1)} all-gather(bf16[8,1792]{1,0:T(8,128)(2,1)S(1)} %multiply_convert_fusion), channel_id=1, replica_groups=mesh['dp_0'=16,'dp_1'=2,'pipe'=8,'tensor'=2] {'dp_1'}, dimensions={0}, use_global_device_ids=true | all-gather | bytes 86016 | tf_op jit(solution)/shard_map/all_gather | solution.py:39
  205.6 32.9 %all_gather.15 = bf16[256,1792]{1,0:T(8,128)(2,1)S(1)} all-gather(bf16[16,1792]{1,0:T(8,128)(2,1)S(1)} %all_gather.14), channel_id=1, replica_groups=mesh['dp_0'=16,'dp_1'=2,'pipe'=8,'tensor'=2] {'dp_0'}, dimensions={0}, use_global_device_ids=true | all-gather | bytes 974848 | tf_op jit(solution)/shard_map/all_gather | solution.py:39
  238.5 0.3 fusion.44
  238.8 0.7 broadcast_in_dim.40
  239.5 3.2 all-to-all-start.4
  242.8 5.3 %all-to-all-done.4 = f32[2,8,256]{2,1,0:T(8,128)S(1)} async-done(((f32[2,8,256]{2,1,0:T(8,128)}), f32[2,8,256]{2,1,0:T(8,128)S(1)}, u32[]{:S(2)}, u32[]{:S(2)}) %all-to-all-start.4) | async-done | bytes 16416 | tf_op jit(solution)/shard_map/all_to_all | solution.py:20
  248.3 0.5 subtract_bitcast_fusion
  248.8 0.6 broadcast_in_dim.42
  249.4 10.4 %all-to-all-start.5 = ((f32[32,1,8]{2,1,0:T(1,128)}), f32[32,1,8]{2,1,0:T(1,128)S(1)}, u32[]{:S(2)}, u32[]{:S(2)}) async-start(f32[32,1,8]{2,1,0:T(1,128)} %broadcast_in_dim.42), calls=%async_computation.5 | async-start | bytes 32768 | tf_op jit(solution)/shard_map/all_to_all | solution.py:20
  260.3 12.6 %all-to-all-done.5 = f32[32,1,8]{2,1,0:T(1,128)S(1)} async-done(((f32[32,1,8]{2,1,0:T(1,128)}), f32[32,1,8]{2,1,0:T(1,128)S(1)}, u32[]{:S(2)}, u32[]{:S(2)}) %all-to-all-start.5) | async-done | bytes 1056 | tf_op jit(solution)/shard_map/all_to_all | solution.py:20
  273.3 0.4 convolution_convert_fusion.1
  273.8 0.4 multiply_reduce_fusion.1
  274.2 1.3 fusion.19
  275.6 0.6 broadcast_in_dim.44
  276.2 3.2 all-to-all-start.6
  279.6 5.1 %all-to-all-done.6 = f32[2,1,264]{2,1,0:T(1,128)S(1)} async-done(((f32[2,1,264]{2,1,0:T(1,128)}), f32[2,1,264]{2,1,0:T(1,128)S(1)}, u32[]{:S(2)}, u32[]{:S(2)}) %all-to-all-start.6) | async-done | bytes 2144 | tf_op jit(solution)/shard_map/all_to_all | solution.py:20
  285.5 0.7 broadcast_in_dim.46
  286.2 3.3 all-to-all-start.8
  289.7 0.5 broadcast.130
  290.2 0.7 reduce.11
  290.9 0.7 reshape.219
  291.5 3.4 all-to-all-done.8
  294.9 3.9 all-to-all-start.9
  298.8 8.9 %convolution_convert_fusion = bf16[128,3584]{1,0:T(8,128)(2,1)S(1)} fusion(bf16[128,1792]{1,0:T(8,128)(2,1)S(1)} %fusion.7, bf16[3584,1792]{1,0:T(8,128)(2,1)} %all-gather.2.cloned.1.call-done), kind=kOutput, calls=%fused_computation | convolution fusion | flops 1644625920 | bytes 14221312 | tf_op jit(solution)/shard_map/dot_general | solution.py:172
  307.7 1.0 copy.75
  308.6 4.7 %all-to-all-done.9 = bf16[32,2,896]{2,1,0:T(2,128)(2,1)S(1)} async-done(((bf16[32,2,896]{2,1,0:T(2,128)(2,1)}), bf16[32,2,896]{2,1,0:T(2,128)(2,1)S(1)}, u32[]{:S(2)}, u32[]{:S(2)}) %all-to-all-start.9) | async-done | bytes 114720 | tf_op jit(solution)/shard_map/all_to_all | solution.py:64
  313.3 3.6 all-to-all-start.7
  317.1 0.7 reduce.13
  317.8 0.7 reshape.223
  318.5 8.9 %all-to-all-done.7 = bf16[2,128,1792]{2,1,0:T(8,128)(2,1)S(1)} async-done(((bf16[2,128,1792]{2,1,0:T(8,128)(2,1)}), bf16[2,128,1792]{2,1,0:T(8,128)(2,1)S(1)}, u32[]{:S(2)}, u32[]{:S(2)}) %all-to-all-start.7) | async-done | bytes 917536 | tf_op jit(solution)/shard_map/all_to_all | solution.py:64
  327.4 8.7 %all-to-all-start.11 = ((bf16[32,2,896]{2,1,0:T(2,128)(2,1)}), bf16[32,2,896]{2,1,0:T(2,128)(2,1)S(1)}, u32[]{:S(2)}, u32[]{:S(2)}) async-start(bf16[32,2,896]{2,1,0:T(2,128)(2,1)} %reshape.223), calls=%async_computation.11 | async-start | bytes 229376 | tf_op jit(solution)/shard_map/all_to_all | solution.py:64
  336.5 1.3 reduce.12
  337.8 0.7 reshape.221
  338.5 13.5 %all-to-all-done.11 = bf16[32,2,896]{2,1,0:T(2,128)(2,1)S(1)} async-done(((bf16[32,2,896]{2,1,0:T(2,128)(2,1)}), bf16[32,2,896]{2,1,0:T(2,128)(2,1)S(1)}, u32[]{:S(2)}, u32[]{:S(2)}) %all-to-all-start.11) | async-done | bytes 114720 | tf_op jit(solution)/shard_map/all_to_all | solution.py:64
  352.0 4.0 %all-to-all-start.10 = ((bf16[32,2,896]{2,1,0:T(2,128)(2,1)}), bf16[32,2,896]{2,1,0:T(2,128)(2,1)S(1)}, u32[]{:S(2)}, u32[]{:S(2)}) async-start(bf16[32,2,896]{2,1,0:T(2,128)(2,1)} %reshape.221), calls=%async_computation.10 | async-start | bytes 229376 | tf_op jit(solution)/shard_map/all_to_all | solution.py:20
  356.2 1.2 fusion.1
  357.9 1.3 reduce.14
  359.2 0.7 reshape.225
  359.9 10.6 %all-to-all-done.10 = bf16[32,2,896]{2,1,0:T(2,128)(2,1)S(1)} async-done(((bf16[32,2,896]{2,1,0:T(2,128)(2,1)}), bf16[32,2,896]{2,1,0:T(2,128)(2,1)S(1)}, u32[]{:S(2)}, u32[]{:S(2)}) %all-to-all-start.10) | async-done | bytes 114720 | tf_op jit(solution)/shard_map/all_to_all | solution.py:20
  370.5 3.9 all-to-all-start.12
  374.7 0.7 copy.59
  375.4 13.7 %all-to-all-done.12 = bf16[32,2,896]{2,1,0:T(2,128)(2,1)S(1)} async-done(((bf16[32,2,896]{2,1,0:T(2,128)(2,1)}), bf16[32,2,896]{2,1,0:T(2,128)(2,1)S(1)}, u32[]{:S(2)}, u32[]{:S(2)}) %all-to-all-start.12) | async-done | bytes 114720 | tf_op jit(solution)/shard_map/all_to_all | solution.py:20
  389.2 0.2 bitcast_convert_fusion
  389.4 0.7 copy.60
  390.1 0.8 copy.80
  (63 shorter events, 4.7 us)
Async XLA Ops:
  7.2 175.3 %copy-start = (bf16[8,32,1792]{2,1,0:T(8,128)(2,1)S(1)}, bf16[8,32,1792]{2,1,0:T(8,128)(2,1)}, u32[]{:S(2)}) copy-start(bf16[8,32,1792]{2,1,0:T(8,128)(2,1)} %param.11) | copy-start | bytes 2752516
  7.2 168.7 %all-gather.2.cloned.1.call-start = ((), (), s32[]{:S(2)}) async-start(), calls=%async_computation.13 | async-start | bytes 13647872 | tf_op jit(solution)/shard_map/all_gather | solution.py:39
  23.6 9.6 %all-to-all-start.1 = ((f32[2,128,32]{1,2,0:T(8,128)}), f32[2,128,32]{1,2,0:T(8,128)S(1)}, u32[]{:S(2)}, u32[]{:S(2)}) async-start(f32[2,128,32]{1,2,0:T(8,128)} %broadcast_in_dim.37), calls=%async_computation.1 | async-start | bytes 65536 | tf_op jit(solution)/shard_map/all_to_all | solution.py:20
  34.2 153.5 %copy-start.4 = (s32[1,256]{1,0:T(1,128)S(1)}, s32[1,256]{1,0:T(1,128)}, u32[]{:S(2)}) copy-start(s32[1,256]{1,0:T(1,128)} %param.12) | copy-start | bytes 3076
  34.3 158.7 %copy-start.3 = (f32[1792]{0:T(1024)S(1)}, f32[1792]{0:T(1024)}, u32[]{:S(2)}) copy-start(f32[1792]{0:T(1024)} %param.9) | copy-start | bytes 21508
  34.3 15.6 %all-to-all-start = ((bf16[2,128,1792]{1,2,0:T(8,128)(2,1)}), bf16[2,128,1792]{1,2,0:T(8,128)(2,1)S(1)}, u32[]{:S(2)}, u32[]{:S(2)}) async-start(bf16[2,128,1792]{1,2,0:T(8,128)(2,1)} %broadcast_in_dim.36), calls=%async_computation | async-start | bytes 1835008 | tf_op jit(solution)/shard_map/all_to_all | solution.py:20
  183.4 9.5 %all-to-all-start.2 = ((f32[2,1,128]{2,1,0:T(1,128)}), f32[2,1,128]{2,1,0:T(1,128)S(1)}, u32[]{:S(2)}, u32[]{:S(2)}) async-start(f32[2,1,128]{2,1,0:T(1,128)} %broadcast_in_dim.38), calls=%async_computation.2 | async-start | bytes 2048 | tf_op jit(solution)/shard_map/all_to_all | solution.py:20
  193.2 66.9 %copy-start.2 = (bf16[128,1792]{1,0:T(8,128)(2,1)}, bf16[128,1792]{1,0:T(8,128)(2,1)S(1)}, u32[]{:S(2)}) copy-start(bf16[128,1792]{1,0:T(8,128)(2,1)S(1)} %get-tuple-element.27) | copy-start | bytes 1376260
  239.5 8.6 %all-to-all-start.4 = ((f32[2,8,256]{2,1,0:T(8,128)}), f32[2,8,256]{2,1,0:T(8,128)S(1)}, u32[]{:S(2)}, u32[]{:S(2)}) async-start(f32[2,8,256]{2,1,0:T(8,128)} %broadcast_in_dim.40), calls=%async_computation.4 | async-start | bytes 32768 | tf_op jit(solution)/shard_map/all_to_all | solution.py:20
  249.4 23.5 %all-to-all-start.5 = ((f32[32,1,8]{2,1,0:T(1,128)}), f32[32,1,8]{2,1,0:T(1,128)S(1)}, u32[]{:S(2)}, u32[]{:S(2)}) async-start(f32[32,1,8]{2,1,0:T(1,128)} %broadcast_in_dim.42), calls=%async_computation.5 | async-start | bytes 32768 | tf_op jit(solution)/shard_map/all_to_all | solution.py:20
  273.3 43.6 %copy-start.1 = (bf16[1,128,1792]{2,1,0:T(8,128)(2,1)S(1)}, bf16[1,128,1792]{2,1,0:T(8,128)(2,1)}, u32[]{:S(2)}) copy-start(bf16[1,128,1792]{2,1,0:T(8,128)(2,1)} %param.7) | copy-start | bytes 1376260
  276.2 8.5 %all-to-all-start.6 = ((f32[2,1,264]{2,1,0:T(1,128)}), f32[2,1,264]{2,1,0:T(1,128)S(1)}, u32[]{:S(2)}, u32[]{:S(2)}) async-start(f32[2,1,264]{2,1,0:T(1,128)} %broadcast_in_dim.44), calls=%async_computation.6 | async-start | bytes 6144 | tf_op jit(solution)/shard_map/all_to_all | solution.py:20
  286.2 8.7 %all-to-all-start.8 = ((f32[2,128,32]{1,2,0:T(8,128)}), f32[2,128,32]{1,2,0:T(8,128)S(1)}, u32[]{:S(2)}, u32[]{:S(2)}) async-start(f32[2,128,32]{1,2,0:T(8,128)} %broadcast_in_dim.46), calls=%async_computation.8 | async-start | bytes 65536 | tf_op jit(solution)/shard_map/all_to_all | solution.py:20
  294.9 18.4 %all-to-all-start.9 = ((bf16[32,2,896]{2,1,0:T(2,128)(2,1)}), bf16[32,2,896]{2,1,0:T(2,128)(2,1)S(1)}, u32[]{:S(2)}, u32[]{:S(2)}) async-start(bf16[32,2,896]{2,1,0:T(2,128)(2,1)} %reshape.219), calls=%async_computation.9 | async-start | bytes 229376 | tf_op jit(solution)/shard_map/all_to_all | solution.py:64
  313.3 14.1 %all-to-all-start.7 = ((bf16[2,128,1792]{2,1,0:T(8,128)(2,1)}), bf16[2,128,1792]{2,1,0:T(8,128)(2,1)S(1)}, u32[]{:S(2)}, u32[]{:S(2)}) async-start(bf16[2,128,1792]{2,1,0:T(8,128)(2,1)} %bitcast.83), calls=%async_computation.7 | async-start | bytes 1835008 | tf_op jit(solution)/shard_map/all_to_all | solution.py:64
  327.4 24.6 %all-to-all-start.11 = ((bf16[32,2,896]{2,1,0:T(2,128)(2,1)}), bf16[32,2,896]{2,1,0:T(2,128)(2,1)S(1)}, u32[]{:S(2)}, u32[]{:S(2)}) async-start(bf16[32,2,896]{2,1,0:T(2,128)(2,1)} %reshape.223), calls=%async_computation.11 | async-start | bytes 229376 | tf_op jit(solution)/shard_map/all_to_all | solution.py:64
  352.0 18.4 %all-to-all-start.10 = ((bf16[32,2,896]{2,1,0:T(2,128)(2,1)}), bf16[32,2,896]{2,1,0:T(2,128)(2,1)S(1)}, u32[]{:S(2)}, u32[]{:S(2)}) async-start(bf16[32,2,896]{2,1,0:T(2,128)(2,1)} %reshape.221), calls=%async_computation.10 | async-start | bytes 229376 | tf_op jit(solution)/shard_map/all_to_all | solution.py:20
  357.4 32.7 %collective-permute-start = (bf16[128,1792]{1,0:T(8,128)(2,1)S(1)}, bf16[128,1792]{1,0:T(8,128)(2,1)S(1)}, u32[]{:S(2)}, u32[]{:S(2)}) collective-permute-start(bf16[128,1792]{1,0:T(8,128)(2,1)S(1)} %fusion.1), channel_id=1, source_target_pairs={{2,0},{4,2},{6,4},{8,6},{10,8},{12,10},{14,12},{0,14},{3,1},{5,3},... | collective-permute-start | bytes 1376264 | tf_op jit(solution)/shard_map/ppermute | solution.py:71
  370.5 18.7 %all-to-all-start.12 = ((bf16[32,2,896]{2,1,0:T(2,128)(2,1)}), bf16[32,2,896]{2,1,0:T(2,128)(2,1)S(1)}, u32[]{:S(2)}, u32[]{:S(2)}) async-start(bf16[32,2,896]{2,1,0:T(2,128)(2,1)} %reshape.225), calls=%async_computation.12 | async-start | bytes 229376 | tf_op jit(solution)/shard_map/all_to_all | solution.py:20
Sparse Core Ops, SparseCore 0:
  21.1 154.7 all-gather.1
where the time goes:
time: 399 us; the launch traced here: 398 us
  waiting for transfers between devices  224 us (56%)
  blocking collectives  58.7 us (15%)
  starting transfers between devices  56.3 us (14%)
  matrix products  21.5 us (5%)
  between operations  15.1 us (4%)
  local copies, waits for them, and re-layouts  14.7 us (4%)
  other arithmetic  7.74 us (2%)
    all_gather x1, waiting for transfers between devices, whole_of(): whole = lax.all_gather(whole, axes[number], axis=dim, tiled=True)  126 us
    all_to_all x9, waiting for transfers between devices, sent_to_all(): lax.all_to_all(jnp.broadcast_to(array[None], (peers, *array.shape)), axis...  70.6 us
    all_gather x3, blocking collectives, whole_of(): whole = lax.all_gather(whole, axes[number], axis=dim, tiled=True)  51.1 us
    all_to_all x9, starting transfers between devices, sent_to_all(): lax.all_to_all(jnp.broadcast_to(array[None], (peers, *array.shape)), axis...  40.1 us
    all_to_all x3, waiting for transfers between devices, sum_at_owner(): parts = lax.all_to_all(split_up(array, dim, peers), axis, 0, 0, tiled=True)  27.1 us
    all_to_all x3, starting transfers between devices, sum_at_owner(): parts = lax.all_to_all(split_up(array, dim, peers), axis, 0, 0, tiled=True)  16.1 us
    dot_general x1, matrix products, body(): lax.dot_general(output_gradient, full_weight, (((1,), (1,)), ((), ())), p...  8.88 us
  transfers between devices with their start and end apart: 14, of which 13 were waited for; matrix products, arithmetic and copies ran while one was open for 7% of the time, Pallas kernels for 0%

commit v1 on v0

v1 whole, which is shorter than its diff:
```python
import jax
import jax.numpy as jnp
from jax import lax
from jax.experimental import pallas as pl
from jax.experimental.pallas import tpu as pltpu
from jax.sharding import PartitionSpec as P

MESH = pl.DeviceIdType.MESH
F32, BF16 = jnp.float32, jnp.bfloat16

WIDTH = 3584
HALF = 1792
CORE = 896
SHARD = 112
PLANE = 224
CUT_A, CUT_B = 48, 96
NZ = 16
SEQ = 16
ROWS = 8
ALL = 256
TOK = 128
RANK = 32
OWNERS = 14
TILE = 256
TILES = 7

logit_divisor = 0.05
loss_scale = 256.0
adapter_scale = 0.5
epsilon = 1e-06


def nt(a, b):
    return lax.dot_general(a, b, (((1,), (1,)), ((), ())), preferred_element_type=F32)


def tn(a, b):
    return lax.dot_general(a, b, (((0,), (0,)), ((), ())), preferred_element_type=F32)


def nn(a, b):
    return jnp.dot(a, b, preferred_element_type=F32)


def per_token(rows):
    width = rows.shape[1]
    return jnp.broadcast_to(rows[:, None, :], (ROWS, SEQ, width)).reshape(TOK, width)


def as_lanes(columns):
    lane = lax.broadcasted_iota(jnp.int32, (TOK, TOK), 1)
    packed = jnp.zeros((TOK, TOK), F32)
    for number, column in enumerate(columns):
        packed = jnp.where(lane == number, jnp.broadcast_to(column, (TOK, TOK)), packed)
    return jnp.transpose(packed)[0:8, :]


def as_columns(lanes):
    return jnp.transpose(lanes)


def kernel(
    x_hbm,
    w_hbm,
    gain_ref,
    down_hbm,
    up_hbm,
    tenant_ref,
    adapter_ref,
    gin_ref,
    gup_ref,
    gdown_ref,
    loss_ref,
    wbuf,
    acc,
    x_own,
    x3,
    downs,
    ups,
    low_snd,
    low_rcv,
    lowt,
    tok_snd,
    tok_rcv,
    pooled_ref,
    e3,
    e2,
    s_snd,
    s_rcv,
    mask_ref,
    sum_snd,
    sum_rcv,
    go,
    gl_snd,
    gl_rcv,
    glt,
    part_snd,
    part_rcv,
    gin_snd,
    rs_up,
    rs_down,
    rs_rcv,
    ag,
    in_sem,
    z_sem,
    xy_sem,
    d2d_sem,
    w_send,
    x_sem,
    small_sem,
    ez_sem,
    ey_sem,
    e_send,
    part_sem,
    gin_sem,
    rs_sem,
    ag_sem,
):
    dp = lax.axis_index("dp")
    pipe = lax.axis_index("pipe")
    tensor = lax.axis_index("tensor")
    z = dp // 2
    y = dp % 2
    x = pipe // 2
    core = pipe % 2
    own_q = (x + y) % 2
    dp_right = (dp + 2) % 32
    dp_left = (dp + 30) % 32
    dp_y = dp + 1 - 2 * y
    x_right = (pipe + 2) % 8
    x_left = (pipe + 6) % 8
    partner = pipe + 1 - 2 * core
    peer = 1 - tensor
    before = (pipe + 7) % 8
    after = (pipe + 1) % 8

    def fetch(src, dst, number):
        return pltpu.make_async_copy(src, dst, in_sem.at[number])

    x_copy = fetch(x_hbm, x_own, 0)
    down_copy = fetch(down_hbm, downs, 1)
    up_copy = fetch(up_hbm, ups, 2)
    x_copy.start()
    down_copy.start()
    up_copy.start()

    barrier = pltpu.get_barrier_semaphore()
    for where in (
        {"dp": dp_right},
        {"dp": dp_left},
        {"dp": dp_y},
        {"pipe": x_right},
        {"pipe": x_left},
        {"pipe": before},
        {"pipe": after},
        {"tensor": peer},
    ):
        pl.semaphore_signal(barrier, inc=1, device_id=where, device_id_type=MESH)
    pl.semaphore_wait(barrier, 8)

    def remote(src, dst, send, recv, where):
        copy = pltpu.make_async_remote_copy(
            src_ref=src, dst_ref=dst, send_sem=send, recv_sem=recv, device_id=where, device_id_type=MESH
        )
        copy.start()

    def arrived(ref, sem):
        pltpu.make_async_copy(ref, ref, sem).wait()

    columns = pl.ds(pl.multiple_of(core * CORE, 128), CORE)

    def piece(zz, q, first, count):
        return wbuf.at[pl.ds(pl.multiple_of((zz * 2 + q) * SHARD + first, 16), count), columns]

    chunks = ((0, CUT_A), (CUT_A, SHARD - CUT_A))

    @pl.when(x % 2 == 0)
    def _():
        for number, (first, count) in enumerate(chunks):
            pltpu.make_async_copy(
                w_hbm.at[pl.ds(first, count), columns], piece(z, own_q, first, count), z_sem.at[0, number]
            ).start()

    @pl.when(x % 2 == 1)
    def _():
        for number, (first, count) in enumerate(chunks):
            remote(
                w_hbm.at[pl.ds(first, count), columns],
                piece(z, y, first, count),
                w_send.at[6],
                z_sem.at[0, number],
                {"dp": dp_y},
            )

    def got(zz, rel, number):
        first, count = chunks[number]
        arrived(piece(zz, own_q, first, count), z_sem.at[rel, number])

    def forward(zz, rel, number, right):
        first, count = chunks[number]
        part = piece(zz, own_q, first, count)
        there = (rel + 15) % NZ if right else (rel + 1) % NZ
        remote(
            part, part, w_send.at[0 if right else 1], z_sem.at[there, number],
            {"dp": dp_right if right else dp_left},
        )

    def share(zz, rel, number):
        if number == 0:
            part = piece(zz, own_q, 0, CUT_A)
            remote(part, part, w_send.at[2], xy_sem.at[rel], {"pipe": x_right})
        else:
            part = piece(zz, own_q, CUT_A, CUT_B - CUT_A)
            remote(part, part, w_send.at[3], xy_sem.at[rel], {"pipe": x_left})
            part = piece(zz, own_q, CUT_B, SHARD - CUT_B)
            remote(part, part, w_send.at[4], xy_sem.at[rel], {"dp": dp_y})
            part = piece(zz, own_q, 0, SHARD)
            remote(part, part, w_send.at[5], d2d_sem.at[0, rel], {"pipe": partner})

    def complement(zz, rel):
        part = piece(zz, 1 - own_q, 0, SHARD)
        arrived(part, xy_sem.at[rel])
        remote(part, part, w_send.at[5], d2d_sem.at[1, rel], {"pipe": partner})

    other = pl.ds(pl.multiple_of((1 - core) * CORE, 128), CORE)

    def compute(zz, rel):
        for number in range(2):
            q = own_q if number == 0 else 1 - own_q
            rows = pl.ds(pl.multiple_of((zz * 2 + q) * SHARD, 16), SHARD)
            arrived(wbuf.at[rows, other], d2d_sem.at[number, rel])
        lhs = x3[zz]
        rows = pl.ds(pl.multiple_of(zz * PLANE, 16), PLANE)
        for n in range(TILES):
            at = slice(n * TILE, (n + 1) * TILE)
            acc[:, at] += nn(lhs, wbuf[rows, at])

    def right_z(k):
        return (z + NZ - k) % NZ

    def left_z(k):
        return (z + k) % NZ

    def prepare():
        x_copy.wait()
        down_copy.wait()
        up_copy.wait()
        for number in range(8):
            x3[tensor * 8 + number] = x_own[:, number * PLANE : (number + 1) * PLANE]
        mine = x3.at[pl.ds(tensor * 8, 8)]
        remote(mine, mine, x_sem.at[0], x_sem.at[1], {"tensor": peer})
        picked = adapter_ref[0]
        low_snd[...] = nt(downs[picked], x_own[...])
        remote(low_snd, low_rcv, small_sem.at[0], small_sem.at[1], {"tensor": peer})
        tenants = jnp.broadcast_to(tenant_ref[...], (ALL, ALL)).astype(F32)
        own = jnp.transpose(tenants)
        row = lax.broadcasted_iota(jnp.int32, (ALL, ALL), 0)
        column = lax.broadcasted_iota(jnp.int32, (ALL, ALL), 1)
        mask_ref[...] = jnp.where((tenants == own) & (row != column), 1.0, 0.0)

    def first_terms():
        arrived(x3.at[pl.ds(peer * 8, 8)], x_sem.at[1])
        arrived(low_rcv, small_sem.at[1])
        picked = adapter_ref[0]
        lowt[...] = (low_snd[...] + low_rcv[...]).astype(BF16)
        for n in range(TILES):
            at = slice(n * TILE, (n + 1) * TILE)
            acc[:, at] = adapter_scale * tn(lowt[...], ups[picked, :, at])

    def step(k, carry):
        rel = (NZ - k) % NZ
        zr = right_z(k)
        zl = left_z(k)

        @pl.when(k <= 8)
        def _():
            got(zr, rel, 0)

        @pl.when(k <= 7)
        def _():
            forward(zr, rel, 0, True)

        @pl.when(k == 0)
        def _():
            forward(z, 0, 0, False)

        @pl.when((k >= 1) & (k <= 7))
        def _():
            got(zl, k, 0)

        @pl.when((k >= 1) & (k <= 6))
        def _():
            forward(zl, k, 0, False)

        @pl.when(k <= 8)
        def _():
            share(zr, rel, 0)

        @pl.when((k >= 1) & (k <= 7))
        def _():
            share(zl, k, 0)

        @pl.when(k <= 8)
        def _():
            got(zr, rel, 1)

        @pl.when(k <= 7)
        def _():
            forward(zr, rel, 1, True)

        @pl.when(k == 0)
        def _():
            forward(z, 0, 1, False)

        @pl.when((k >= 1) & (k <= 7))
        def _():
            got(zl, k, 1)

        @pl.when((k >= 1) & (k <= 6))
        def _():
            forward(zl, k, 1, False)

        @pl.when(k <= 8)
        def _():
            share(zr, rel, 1)

        @pl.when((k >= 1) & (k <= 7))
        def _():
            share(zl, k, 1)

        @pl.when(k == 0)
        def _():
            prepare()

        @pl.when((k >= 1) & (k <= 9))
        def _():
            complement(right_z(k - 1), (NZ + 1 - k) % NZ)

        @pl.when((k >= 2) & (k <= 8))
        def _():
            complement(left_z(k - 1), k - 1)

        @pl.when(k == 2)
        def _():
            first_terms()

        @pl.when(k >= 2)
        def _():
            compute(right_z(k - 2), (NZ + 2 - k) % NZ)

        @pl.when((k >= 3) & (k <= 9))
        def _():
            compute(left_z(k - 2), k - 2)

        return carry

    lax.fori_loop(0, 11, step, 0)

    picked = adapter_ref[0]

    out = acc[...]
    tok_snd[...] = as_lanes((jnp.sum(out * out, axis=1, keepdims=True),))
    remote(tok_snd, tok_rcv, small_sem.at[2], small_sem.at[3], {"tensor": peer})
    arrived(tok_rcv, small_sem.at[3])
    squares = as_columns(tok_snd[...] + tok_rcv[...])[:, 0:1]
    token_inv = lax.rsqrt(squares / WIDTH + epsilon)
    gained = acc[...] * gain_ref[...]
    pooled = jnp.sum((gained * token_inv).reshape(ROWS, SEQ, HALF), axis=1) * (1.0 / SEQ)
    pooled_ref[...] = pooled
    e3[dp] = pooled.astype(BF16)

    def row_of(zz, yy):
        return e3.at[zz * 2 + yy]

    def e_forward(zz, rel, right):
        there = (rel + 15) % NZ if right else (rel + 1) % NZ
        part = row_of(zz, y)
        remote(
            part, part, e_send.at[0 if right else 1], ez_sem.at[there],
            {"dp": dp_right if right else dp_left},
        )

    def e_share(zz, rel):
        part = row_of(zz, y)
        remote(part, part, e_send.at[2], ey_sem.at[rel], {"dp": dp_y})

    e_forward(z, 0, True)
    e_forward(z, 0, False)
    e_share(z, 0)
    second = jnp.sum(acc[...] * gain_ref[...] * per_token(pooled_ref[...]), axis=1, keepdims=True)

    def e_step(k, carry):
        rel = (NZ - k) % NZ
        arrived(row_of(right_z(k), y), ez_sem.at[rel])

        @pl.when(k <= 7)
        def _():
            e_forward(right_z(k), rel, True)

        @pl.when(k <= 7)
        def _():
            arrived(row_of(left_z(k), y), ez_sem.at[k])

        @pl.when(k <= 6)
        def _():
            e_forward(left_z(k), k, False)

        e_share(right_z(k), rel)

        @pl.when(k <= 7)
        def _():
            e_share(left_z(k), k)

        return carry

    lax.fori_loop(1, 9, e_step, 0)

    def e_last(rel, carry):
        arrived(row_of((z + rel) % NZ, 1 - y), ey_sem.at[rel])
        return carry

    lax.fori_loop(0, NZ, e_last, 0)
    e2[...] = e3[...].astype(F32).reshape(ALL, HALF).astype(BF16)

    s_snd[...] = nt(e2[...], e2[...])
    remote(s_snd, s_rcv, small_sem.at[4], small_sem.at[5], {"tensor": peer})
    arrived(s_rcv, small_sem.at[5])
    row = lax.broadcasted_iota(jnp.int32, (ALL, ALL), 0)
    column = lax.broadcasted_iota(jnp.int32, (ALL, ALL), 1)
    raw = s_snd[...] + s_rcv[...]
    diagonal = jnp.where(row == column, raw, 0.0)
    inverse_row = lax.rsqrt(jnp.sum(diagonal, axis=0, keepdims=True) + epsilon)
    inverse_column = lax.rsqrt(jnp.sum(diagonal, axis=1, keepdims=True) + epsilon)
    scores = raw * inverse_column * inverse_row / logit_divisor
    exps = jnp.where(mask_ref[...] > 0.0, jnp.exp(scores), 0.0)
    total_row = jnp.log(jnp.sum(exps, axis=0, keepdims=True))
    s_snd_rows = pl.ds(pl.multiple_of(dp * ROWS, ROWS), ROWS)
    own_raw = s_snd[s_snd_rows, :] + s_rcv[s_snd_rows, :]
    own_mask = mask_ref[s_snd_rows, :]
    own_row = lax.broadcasted_iota(jnp.int32, (ROWS, ALL), 0) + dp * ROWS
    own_column = lax.broadcasted_iota(jnp.int32, (ROWS, ALL), 1)
    inverse = lax.rsqrt(
        jnp.sum(jnp.where(own_row == own_column, own_raw, 0.0), axis=1, keepdims=True) + epsilon
    )
    own_scores = own_raw * inverse * inverse_row / logit_divisor
    mated = own_column == own_row + 1 - 2 * (own_row % 2)
    allowed = own_mask > 0.0
    total = jnp.log(jnp.sum(jnp.where(allowed, jnp.exp(own_scores), 0.0), axis=1, keepdims=True))
    positive = jnp.sum(jnp.where(mated, own_scores, 0.0), axis=1, keepdims=True)
    loss = jnp.broadcast_to(total - positive, (ROWS, TOK))
    loss_ref[...] = jnp.transpose(loss)[0:1, :]
    both = jnp.where(allowed, jnp.exp(own_scores - total) + jnp.exp(own_scores - total_row), 0.0)
    weights = loss_scale * (both - jnp.where(mated, 2.0, 0.0))
    grad_emb = nn((weights * inverse_row).astype(BF16), e2[...]) / logit_divisor

    unit = pooled_ref[...] * inverse
    along_part = jnp.sum(unit * grad_emb, axis=1, keepdims=True)
    gained = acc[...] * gain_ref[...]
    first = jnp.sum(gained * per_token(grad_emb), axis=1, keepdims=True)
    along_tokens = per_token(jnp.broadcast_to(along_part, (ROWS, TOK)))[:, 0:1]
    sum_snd[...] = as_lanes((first, second, along_tokens))
    remote(sum_snd, sum_rcv, small_sem.at[6], small_sem.at[7], {"tensor": peer})
    arrived(sum_rcv, small_sem.at[7])
    sums = as_columns(sum_snd[...] + sum_rcv[...])
    first_sum, second_sum, along = sums[:, 0:1], sums[:, 1:2], sums[:, 2:3]
    inverse_tokens = per_token(jnp.broadcast_to(inverse, (ROWS, TOK)))[:, 0:1]
    inner = inverse_tokens * (first_sum - along * inverse_tokens * second_sum) * (1.0 / SEQ)
    spread = (
        inverse_tokens
        * (per_token(grad_emb) - per_token(unit) * along)
        * gain_ref[...]
        * (1.0 / SEQ)
    )
    pull = inner * token_inv * token_inv * (1.0 / WIDTH)
    go[...] = (token_inv * (spread - acc[...] * pull)).astype(BF16)

    gl_snd[...] = adapter_scale * nt(ups[picked], go[...])
    remote(gl_snd, gl_rcv, small_sem.at[8], small_sem.at[9], {"tensor": peer})

    owner = z < OWNERS

    def scatter(buffer, values, kind):
        for number in range(OWNERS):
            buffer[number] = values[:, number * 128 : (number + 1) * 128].astype(BF16)

        @pl.when((y == kind) & owner)
        def _():
            rs_rcv[dp] = buffer[jnp.minimum(z, OWNERS - 1)]

        def one(off, carry):
            zz = (z + off) % NZ
            there = zz * 2 + kind

            @pl.when((zz < OWNERS) & (there != dp))
            def _():
                remote(
                    buffer.at[zz], rs_rcv.at[dp], rs_sem.at[kind], rs_sem.at[2], {"dp": there}
                )

            return carry

        lax.fori_loop(0, NZ, one, 0)

    scatter(rs_up, adapter_scale * nn(lowt[...], go[...]), 0)

    def part_step(j, carry):
        rows = pl.ds(pl.multiple_of(peer * HALF + j * TILE, TILE), TILE)
        part_snd[j] = nt(go[...], wbuf[rows, :]).astype(BF16)
        remote(part_snd.at[j], part_rcv.at[j], part_sem.at[TILES], part_sem.at[j], {"tensor": peer})
        return carry

    lax.fori_loop(0, TILES, part_step, 0)

    arrived(gl_rcv, small_sem.at[9])
    glt[...] = (gl_snd[...] + gl_rcv[...]).astype(BF16)
    scatter(rs_down, nn(glt[...], x_own[...]), 1)

    def gin_step(j, carry):
        rows = pl.ds(pl.multiple_of(tensor * HALF + j * TILE, TILE), TILE)
        at = pl.ds(pl.multiple_of(j * TILE, TILE), TILE)
        mine = nt(go[...], wbuf[rows, :]) + tn(glt[...], downs[picked, :, at])
        arrived(part_rcv.at[j], part_sem.at[j])
        gin_snd[j] = (mine + part_rcv[j].astype(F32)).astype(BF16)
        remote(gin_snd.at[j], gin_ref.at[:, at], gin_sem.at[TILES], gin_sem.at[j], {"pipe": before})
        return carry

    lax.fori_loop(0, TILES, gin_step, 0)

    @pl.when(owner)
    def _():
        arrived(rs_rcv.at[pl.ds(0, 31)], rs_sem.at[2])
        mine = ag.at[y * OWNERS + jnp.minimum(z, OWNERS - 1)]
        mine[...] = jnp.sum(rs_rcv[...].astype(F32), axis=0).astype(BF16)

        def one(off, carry):
            remote(mine, mine, ag_sem.at[0], ag_sem.at[1], {"dp": (dp + off) % 32})
            return carry

        lax.fori_loop(1, 32, one, 0)
        arrived(ag.at[pl.ds(0, 2 * OWNERS - 1)], ag_sem.at[1])

    @pl.when(z >= OWNERS)
    def _():
        arrived(ag, ag_sem.at[1])

    for number in range(OWNERS):
        at = slice(number * 128, (number + 1) * 128)
        gup_ref[:, at] = ag[number].astype(F32)
        gdown_ref[:, at] = ag[OWNERS + number].astype(F32)

    for number, rows in enumerate((8 * SHARD, 7 * SHARD, NZ * 48, NZ * 48, NZ * 16, 2 * NZ * SHARD)):
        arrived(wbuf.at[pl.ds(0, rows), pl.ds(0, CORE)], w_send.at[number])

    @pl.when(x % 2 == 1)
    def _():
        arrived(wbuf.at[pl.ds(0, SHARD), pl.ds(0, CORE)], w_send.at[6])

    arrived(x3.at[pl.ds(0, 8)], x_sem.at[0])
    arrived(low_snd, small_sem.at[0])
    arrived(tok_snd, small_sem.at[2])
    arrived(e3.at[pl.ds(0, 8)], e_send.at[0])
    arrived(e3.at[pl.ds(0, 7)], e_send.at[1])
    arrived(e3.at[pl.ds(0, 16)], e_send.at[2])
    arrived(s_snd, small_sem.at[4])
    arrived(sum_snd, small_sem.at[6])
    arrived(gl_snd, small_sem.at[8])
    arrived(part_snd, part_sem.at[TILES])
    arrived(gin_snd, gin_sem.at[TILES])
    for kind in range(2):

        @pl.when((y == kind) & owner)
        def _():
            arrived(rs_up.at[pl.ds(0, OWNERS - 1)], rs_sem.at[kind])

        @pl.when((y != kind) | (z >= OWNERS))
        def _():
            arrived(rs_up, rs_sem.at[kind])

    @pl.when(owner)
    def _():
        arrived(rs_rcv.at[pl.ds(0, 31)], ag_sem.at[0])

    def gin_last(j, carry):
        at = pl.ds(pl.multiple_of(j * TILE, TILE), TILE)
        arrived(gin_ref.at[:, at], gin_sem.at[j])
        return carry

    lax.fori_loop(0, TILES, gin_last, 0)


def body(hidden, frozen_weight, final_norm_gain, down_maps, up_maps, tenant, adapter):
    vmem = pl.BlockSpec(memory_space=pltpu.VMEM)
    anywhere = pl.BlockSpec(memory_space=pl.ANY)
    dma = pltpu.SemaphoreType.DMA
    gin, gup, gdown, loss = pl.pallas_call(
        kernel,
        name="whole_step",
        out_shape=(
            jax.ShapeDtypeStruct((TOK, HALF), BF16),
            jax.ShapeDtypeStruct((RANK, HALF), F32),
            jax.ShapeDtypeStruct((RANK, HALF), F32),
            jax.ShapeDtypeStruct((1, ROWS), F32),
        ),
        in_specs=[
            anywhere,
            anywhere,
            vmem,
            anywhere,
            anywhere,
            vmem,
            pl.BlockSpec(memory_space=pltpu.SMEM),
        ],
        out_specs=(anywhere, vmem, vmem, vmem),
        scratch_shapes=[
            pltpu.VMEM((WIDTH, HALF), BF16),
            pltpu.VMEM((TOK, HALF), F32),
            pltpu.VMEM((TOK, HALF), BF16),
            pltpu.VMEM((NZ, TOK, PLANE), BF16),
            pltpu.VMEM((8, RANK, HALF), BF16),
            pltpu.VMEM((8, RANK, HALF), BF16),
            pltpu.VMEM((RANK, TOK), F32),
            pltpu.VMEM((RANK, TOK), F32),
            pltpu.VMEM((RANK, TOK), BF16),
            pltpu.VMEM((8, TOK), F32),
            pltpu.VMEM((8, TOK), F32),
            pltpu.VMEM((ROWS, HALF), F32),
            pltpu.VMEM((32, ROWS, HALF), BF16),
            pltpu.VMEM((ALL, HALF), BF16),
            pltpu.VMEM((ALL, ALL), F32),
            pltpu.VMEM((ALL, ALL), F32),
            pltpu.VMEM((ALL, ALL), F32),
            pltpu.VMEM((8, TOK), F32),
            pltpu.VMEM((8, TOK), F32),
            pltpu.VMEM((TOK, HALF), BF16),
            pltpu.VMEM((RANK, TOK), F32),
            pltpu.VMEM((RANK, TOK), F32),
            pltpu.VMEM((RANK, TOK), BF16),
            pltpu.VMEM((TILES, TOK, TILE), BF16),
            pltpu.VMEM((TILES, TOK, TILE), BF16),
            pltpu.VMEM((TILES, TOK, TILE), BF16),
            pltpu.VMEM((OWNERS, RANK, 128), BF16),
            pltpu.VMEM((OWNERS, RANK, 128), BF16),
            pltpu.VMEM((32, RANK, 128), BF16),
            pltpu.VMEM((2 * OWNERS, RANK, 128), BF16),
            dma((3,)),
            dma((NZ, 2)),
            dma((NZ,)),
            dma((2, NZ)),
            dma((7,)),
            dma((2,)),
            dma((10,)),
            dma((NZ,)),
            dma((NZ,)),
            dma((3,)),
            dma((TILES + 1,)),
            dma((TILES + 1,)),
            dma((3,)),
            dma((2,)),
        ],
        compiler_params=pltpu.CompilerParams(
            collective_id=0, has_side_effects=True, vmem_limit_bytes=56 * 1024 * 1024
        ),
    )(hidden[0], frozen_weight, final_norm_gain[None, :], down_maps, up_maps, tenant, adapter)
    return gin[None], gup[None], gdown[None], loss


def solution(mesh):
    return jax.shard_map(
        body,
        mesh=mesh,
        in_specs=(
            P("pipe", "dp", "tensor"),
            P("dp", "tensor"),
            P("tensor"),
            P(None, None, "tensor"),
            P(None, None, "tensor"),
            P("pipe", None),
            P("pipe"),
        ),
        out_specs=(
            P("pipe", "dp", "tensor"),
            P("pipe", None, "tensor"),
            P("pipe", None, "tensor"),
            P("pipe", "dp"),
        ),
        check_vma=False,
    )
```

time: 399 us -> 145 us (0.36)
  the two profiles are of different devices: /device:TPU:2 before, /device:TPU:6 now
where the time goes in v1:
time: 145 us
  Pallas kernels  138 us (95%)
  local copies, waits for them, and re-layouts  5.38 us (4%)
    pallas_call x1, Pallas kernels, body(): pl.pallas_call(kernel, name='whole_step', out_shape=(jax.ShapeDtypeStruct...  138 us
    unnamed x10, local copies, waits for them, and re-layouts  4.08 us

profile of v1, /device:TPU:6, one launch (start us, length us, event | category | flops | bytes accessed | tf_op | source)
XLA Modules:
  0.0 144.7 jit_solution(10950779865931674134)
XLA Ops:
  1.3 1.3 broadcast_in_dim.12.gain_ref
  2.6 138.1 %whole_step.1 = (bf16[128,1792]{1,0:T(8,128)(2,1)}, f32[32,1792]{1,0:T(8,128)}, f32[32,1792]{1,0:T(8,128)}, f32[1,8]{1,0:T(1,128)}) custom-call(bf16[128,1792]{1,0:T(8,128)(2,1)} %bitcast.5, bf16[112,1792]{1,0:T(8,128)(2,1)} %w_hbm.1, f32[1,1792]{1,0:T(1,128)} %broadcast_in_dim.12.gain_ref, bf16[8,32,1792]{2,1,0:T(8,128)(2,1)} %down_hbm.1, ...), custom_call_target="tpu_custom_call" | custom-call | tf_op jit(solution)/shard_map/whole_step/pallas_call | solution.py:595
  140.6 0.0 copy-start.1
  140.7 1.9 %copy.16 = bf16[1,128,1792]{2,1,0:T(8,128)(2,1)} copy(bf16[1,128,1792]{2,1,0:T(8,128)(2,1)} %bitcast.4) | data formatting | bytes 917504
  142.5 0.0 copy-done.1
  142.5 0.0 copy-start
  142.5 0.7 copy.17
  143.2 0.3 copy-done
  143.5 0.0 copy-start.2
  143.5 0.7 copy.18
  144.2 0.0 copy-done.2
  144.2 0.5 copy.19
Async XLA Ops:
  140.6 1.9 %copy-start.1 = (f32[32,1792]{1,0:T(8,128)S(1)}, f32[32,1792]{1,0:T(8,128)}, u32[]{:S(2)}) copy-start(f32[32,1792]{1,0:T(8,128)} %get-tuple-element.9) | copy-start | bytes 688132
  142.5 1.0 copy-start
  143.5 0.7 copy-start.2

commit v2 on v1

--- a/solution.py
+++ b/solution.py
@@ -62,7 +62,7 @@
 def kernel(
     x_hbm,
     w_hbm,
-    gain_ref,
+    gain_hbm,
     down_hbm,
     up_hbm,
     tenant_ref,
@@ -71,6 +71,7 @@
     gup_ref,
     gdown_ref,
     loss_ref,
+    gain_ref,
     wbuf,
     acc,
     x_own,
@@ -87,6 +88,7 @@
     e2,
     s_snd,
     s_rcv,
+    s_all,
     mask_ref,
     sum_snd,
     sum_rcv,
@@ -96,6 +98,7 @@
     glt,
     part_snd,
     part_rcv,
+    own_part,
     gin_snd,
     rs_up,
     rs_down,
@@ -143,6 +146,8 @@
     x_copy.start()
     down_copy.start()
     up_copy.start()
+    gain_copy = fetch(gain_hbm, gain_ref.at[0], 3)
+    gain_copy.start()
 
     barrier = pltpu.get_barrier_semaphore()
     for where in (
@@ -245,6 +250,7 @@
         x_copy.wait()
         down_copy.wait()
         up_copy.wait()
+        gain_copy.wait()
         for number in range(8):
             x3[tensor * 8 + number] = x_own[:, number * PLANE : (number + 1) * PLANE]
         mine = x3.at[pl.ds(tensor * 8, 8)]
@@ -272,61 +278,35 @@
         zr = right_z(k)
         zl = left_z(k)
 
-        @pl.when(k <= 8)
-        def _():
-            got(zr, rel, 0)
-
-        @pl.when(k <= 7)
-        def _():
-            forward(zr, rel, 0, True)
-
-        @pl.when(k == 0)
-        def _():
-            forward(z, 0, 0, False)
-
-        @pl.when((k >= 1) & (k <= 7))
-        def _():
-            got(zl, k, 0)
-
-        @pl.when((k >= 1) & (k <= 6))
-        def _():
-            forward(zl, k, 0, False)
-
-        @pl.when(k <= 8)
-        def _():
-            share(zr, rel, 0)
-
-        @pl.when((k >= 1) & (k <= 7))
-        def _():
-            share(zl, k, 0)
-
-        @pl.when(k <= 8)
-        def _():
-            got(zr, rel, 1)
-
-        @pl.when(k <= 7)
-        def _():
-            forward(zr, rel, 1, True)
-
-        @pl.when(k == 0)
-        def _():
-            forward(z, 0, 1, False)
-
-        @pl.when((k >= 1) & (k <= 7))
-        def _():
-            got(zl, k, 1)
-
-        @pl.when((k >= 1) & (k <= 6))
-        def _():
-            forward(zl, k, 1, False)
-
-        @pl.when(k <= 8)
-        def _():
-            share(zr, rel, 1)
-
-        @pl.when((k >= 1) & (k <= 7))
-        def _():
-            share(zl, k, 1)
+        for number in range(2):
+
+            @pl.when(k <= 8)
+            def _():
+                got(zr, rel, number)
+
+            @pl.when(k <= 7 - number)
+            def _():
+                forward(zr, rel, number, True)
+
+            @pl.when(k == 0)
+            def _():
+                forward(z, 0, number, False)
+
+            @pl.when((k >= 1) & (k <= 7))
+            def _():
+                got(zl, k, number)
+
+            @pl.when((k >= 1) & (k <= 6 + number))
+            def _():
+                forward(zl, k, number, False)
+
+            @pl.when(k <= 8)
+            def _():
+                share(zr, rel, number)
+
+            @pl.when((k >= 1) & (k <= 7))
+            def _():
+                share(zl, k, number)
 
         @pl.when(k == 0)
         def _():
@@ -369,74 +349,79 @@
     pooled_ref[...] = pooled
     e3[dp] = pooled.astype(BF16)
 
-    def row_of(zz, yy):
-        return e3.at[zz * 2 + yy]
-
-    def e_forward(zz, rel, right):
-        there = (rel + 15) % NZ if right else (rel + 1) % NZ
-        part = row_of(zz, y)
+    def row_of(rel, yy):
+        return e3.at[((z + rel) % NZ) * 2 + yy]
+
+    def e_send_z(rel, hops, half=None):
+        part = row_of(rel, y)
+        if half is not None:
+            part = part.at[:, pl.ds(half * CORE, CORE)]
         remote(
-            part, part, e_send.at[0 if right else 1], ez_sem.at[there],
-            {"dp": dp_right if right else dp_left},
+            part, part, e_send.at[0], ez_sem.at[(rel - hops) % NZ], {"dp": (dp + 32 + 2 * hops) % 32}
         )
 
-    def e_share(zz, rel):
-        part = row_of(zz, y)
-        remote(part, part, e_send.at[2], ey_sem.at[rel], {"dp": dp_y})
-
-    e_forward(z, 0, True)
-    e_forward(z, 0, False)
-    e_share(z, 0)
+    def e_send_y(rel):
+        part = row_of(rel, y)
+        remote(part, part, e_send.at[1], ey_sem.at[rel], {"dp": dp_y})
+
+    for hops in (4, -4, 1, -1, 2, -2):
+        e_send_z(0, hops)
+    e_send_y(0)
     second = jnp.sum(acc[...] * gain_ref[...] * per_token(pooled_ref[...]), axis=1, keepdims=True)
-
-    def e_step(k, carry):
-        rel = (NZ - k) % NZ
-        arrived(row_of(right_z(k), y), ez_sem.at[rel])
-
-        @pl.when(k <= 7)
-        def _():
-            e_forward(right_z(k), rel, True)
-
-        @pl.when(k <= 7)
-        def _():
-            arrived(row_of(left_z(k), y), ez_sem.at[k])
-
-        @pl.when(k <= 6)
-        def _():
-            e_forward(left_z(k), k, False)
-
-        e_share(right_z(k), rel)
-
-        @pl.when(k <= 7)
-        def _():
-            e_share(left_z(k), k)
-
-        return carry
-
-    lax.fori_loop(1, 9, e_step, 0)
+    for rel in (15, 1, 14, 2, 12, 4, 11, 3, 13, 5, 10, 6, 8, 7, 9):
+        arrived(row_of(rel, y), ez_sem.at[rel])
+        if rel == 12:
+            e_send_z(12, 4, 0)
+        if rel == 4:
+            e_send_z(4, -4, 1)
+        if rel % 4 == 0:
+            e_send_z(rel, 1)
+            e_send_z(rel, -1)
+        if rel == 12:
+            e_send_z(12, 2)
+        if rel == 4:
+            e_send_z(4, -2)
+        e_send_y(rel)
 
     def e_last(rel, carry):
-        arrived(row_of((z + rel) % NZ, 1 - y), ey_sem.at[rel])
+        arrived(e3.at[((z + rel) % NZ) * 2 + 1 - y], ey_sem.at[rel])
         return carry
 
     lax.fori_loop(0, NZ, e_last, 0)
     e2[...] = e3[...].astype(F32).reshape(ALL, HALF).astype(BF16)
 
-    s_snd[...] = nt(e2[...], e2[...])
+    row = lax.broadcasted_iota(jnp.int32, (TOK, TOK), 0)
+    column = lax.broadcasted_iota(jnp.int32, (TOK, TOK), 1)
+    upper, lower = e2[0:TOK, :], e2[TOK:ALL, :]
+    corner = nt(lower, lower)
+    s_snd[0:TOK, :] = nt(upper, lower)
+    s_snd[TOK:ALL, :] = jnp.where(row >= column, nt(upper, upper), corner)
+    s_snd[ALL:, :] = jnp.broadcast_to(
+        jnp.sum(jnp.where(row == column, corner, 0.0), axis=0, keepdims=True), (8, TOK)
+    )
     remote(s_snd, s_rcv, small_sem.at[4], small_sem.at[5], {"tensor": peer})
     arrived(s_rcv, small_sem.at[5])
+    block = s_snd[0:TOK, :] + s_rcv[0:TOK, :]
+    both = s_snd[TOK:ALL, :] + s_rcv[TOK:ALL, :]
+    below = jnp.where(row > column, both, 0.0)
+    above = jnp.where(row < column, both, 0.0)
+    corner = jnp.broadcast_to(s_snd[ALL : ALL + 1, :] + s_rcv[ALL : ALL + 1, :], (TOK, TOK))
+    s_all[0:TOK, 0:TOK] = jnp.where(row >= column, both, 0.0) + jnp.transpose(below)
+    s_all[0:TOK, TOK:ALL] = block
+    s_all[TOK:ALL, 0:TOK] = jnp.transpose(block)
+    s_all[TOK:ALL, TOK:ALL] = above + jnp.transpose(above) + jnp.where(row == column, corner, 0.0)
     row = lax.broadcasted_iota(jnp.int32, (ALL, ALL), 0)
     column = lax.broadcasted_iota(jnp.int32, (ALL, ALL), 1)
-    raw = s_snd[...] + s_rcv[...]
+    raw = s_all[...]
     diagonal = jnp.where(row == column, raw, 0.0)
     inverse_row = lax.rsqrt(jnp.sum(diagonal, axis=0, keepdims=True) + epsilon)
     inverse_column = lax.rsqrt(jnp.sum(diagonal, axis=1, keepdims=True) + epsilon)
     scores = raw * inverse_column * inverse_row / logit_divisor
     exps = jnp.where(mask_ref[...] > 0.0, jnp.exp(scores), 0.0)
     total_row = jnp.log(jnp.sum(exps, axis=0, keepdims=True))
-    s_snd_rows = pl.ds(pl.multiple_of(dp * ROWS, ROWS), ROWS)
-    own_raw = s_snd[s_snd_rows, :] + s_rcv[s_snd_rows, :]
-    own_mask = mask_ref[s_snd_rows, :]
+    own_rows = pl.ds(pl.multiple_of(dp * ROWS, ROWS), ROWS)
+    own_raw = s_all[own_rows, :]
+    own_mask = mask_ref[own_rows, :]
     own_row = lax.broadcasted_iota(jnp.int32, (ROWS, ALL), 0) + dp * ROWS
     own_column = lax.broadcasted_iota(jnp.int32, (ROWS, ALL), 1)
     inverse = lax.rsqrt(
@@ -509,22 +494,21 @@
         remote(part_snd.at[j], part_rcv.at[j], part_sem.at[TILES], part_sem.at[j], {"tensor": peer})
         return carry
 
-    lax.fori_loop(0, TILES, part_step, 0)
+    lax.fori_loop(0, 3, part_step, 0)
 
     arrived(gl_rcv, small_sem.at[9])
     glt[...] = (gl_snd[...] + gl_rcv[...]).astype(BF16)
     scatter(rs_down, nn(glt[...], x_own[...]), 1)
 
-    def gin_step(j, carry):
+    lax.fori_loop(3, TILES, part_step, 0)
+
+    def own_step(j, carry):
         rows = pl.ds(pl.multiple_of(tensor * HALF + j * TILE, TILE), TILE)
         at = pl.ds(pl.multiple_of(j * TILE, TILE), TILE)
-        mine = nt(go[...], wbuf[rows, :]) + tn(glt[...], downs[picked, :, at])
-        arrived(part_rcv.at[j], part_sem.at[j])
-        gin_snd[j] = (mine + part_rcv[j].astype(F32)).astype(BF16)
-        remote(gin_snd.at[j], gin_ref.at[:, at], gin_sem.at[TILES], gin_sem.at[j], {"pipe": before})
+        own_part[j] = nt(go[...], wbuf[rows, :]) + tn(glt[...], downs[picked, :, at])
         return carry
 
-    lax.fori_loop(0, TILES, gin_step, 0)
+    lax.fori_loop(0, TILES, own_step, 0)
 
     @pl.when(owner)
     def _():
@@ -537,6 +521,18 @@
             return carry
 
         lax.fori_loop(1, 32, one, 0)
+
+    def gin_step(j, carry):
+        at = pl.ds(pl.multiple_of(j * TILE, TILE), TILE)
+        arrived(part_rcv.at[j], part_sem.at[j])
+        gin_snd[j] = (own_part[j] + part_rcv[j].astype(F32)).astype(BF16)
+        remote(gin_snd.at[j], gin_ref.at[:, at], gin_sem.at[TILES], gin_sem.at[j], {"pipe": before})
+        return carry
+
+    lax.fori_loop(0, TILES, gin_step, 0)
+
+    @pl.when(owner)
+    def _():
         arrived(ag.at[pl.ds(0, 2 * OWNERS - 1)], ag_sem.at[1])
 
     @pl.when(z >= OWNERS)
@@ -548,7 +544,7 @@
         gup_ref[:, at] = ag[number].astype(F32)
         gdown_ref[:, at] = ag[OWNERS + number].astype(F32)
 
-    for number, rows in enumerate((8 * SHARD, 7 * SHARD, NZ * 48, NZ * 48, NZ * 16, 2 * NZ * SHARD)):
+    for number, rows in enumerate((7 * SHARD + CUT_A, 8 * SHARD - CUT_A, NZ * 48, NZ * 48, NZ * 16, 2 * NZ * SHARD)):
         arrived(wbuf.at[pl.ds(0, rows), pl.ds(0, CORE)], w_send.at[number])
 
     @pl.when(x % 2 == 1)
@@ -558,9 +554,8 @@
     arrived(x3.at[pl.ds(0, 8)], x_sem.at[0])
     arrived(low_snd, small_sem.at[0])
     arrived(tok_snd, small_sem.at[2])
-    arrived(e3.at[pl.ds(0, 8)], e_send.at[0])
-    arrived(e3.at[pl.ds(0, 7)], e_send.at[1])
-    arrived(e3.at[pl.ds(0, 16)], e_send.at[2])
+    arrived(e3.at[pl.ds(0, 15)], e_send.at[0])
+    arrived(e3.at[pl.ds(0, 16)], e_send.at[1])
     arrived(s_snd, small_sem.at[4])
     arrived(sum_snd, small_sem.at[6])
     arrived(gl_snd, small_sem.at[8])
@@ -596,15 +591,15 @@
         kernel,
         name="whole_step",
         out_shape=(
-            jax.ShapeDtypeStruct((TOK, HALF), BF16),
-            jax.ShapeDtypeStruct((RANK, HALF), F32),
-            jax.ShapeDtypeStruct((RANK, HALF), F32),
-            jax.ShapeDtypeStruct((1, ROWS), F32),
+            pltpu.VMEM((TOK, HALF), BF16),
+            pltpu.VMEM((RANK, HALF), F32),
+            pltpu.VMEM((RANK, HALF), F32),
+            pltpu.VMEM((1, ROWS), F32),
         ),
         in_specs=[
             anywhere,
             anywhere,
-            vmem,
+            anywhere,
             anywhere,
             anywhere,
             vmem,
@@ -612,6 +607,7 @@
         ],
         out_specs=(anywhere, vmem, vmem, vmem),
         scratch_shapes=[
+            pltpu.VMEM((1, HALF), F32),
             pltpu.VMEM((WIDTH, HALF), BF16),
             pltpu.VMEM((TOK, HALF), F32),
             pltpu.VMEM((TOK, HALF), BF16),
@@ -626,7 +622,8 @@
             pltpu.VMEM((ROWS, HALF), F32),
             pltpu.VMEM((32, ROWS, HALF), BF16),
             pltpu.VMEM((ALL, HALF), BF16),
-            pltpu.VMEM((ALL, ALL), F32),
+            pltpu.VMEM((ALL + 8, TOK), F32),
+            pltpu.VMEM((ALL + 8, TOK), F32),
             pltpu.VMEM((ALL, ALL), F32),
             pltpu.VMEM((ALL, ALL), F32),
             pltpu.VMEM((8, TOK), F32),
@@ -637,12 +634,13 @@
             pltpu.VMEM((RANK, TOK), BF16),
             pltpu.VMEM((TILES, TOK, TILE), BF16),
             pltpu.VMEM((TILES, TOK, TILE), BF16),
+            pltpu.VMEM((TILES, TOK, TILE), F32),
             pltpu.VMEM((TILES, TOK, TILE), BF16),
             pltpu.VMEM((OWNERS, RANK, 128), BF16),
             pltpu.VMEM((OWNERS, RANK, 128), BF16),
             pltpu.VMEM((32, RANK, 128), BF16),
             pltpu.VMEM((2 * OWNERS, RANK, 128), BF16),
-            dma((3,)),
+            dma((4,)),
             dma((NZ, 2)),
             dma((NZ,)),
             dma((2, NZ)),
@@ -651,7 +649,7 @@
             dma((10,)),
             dma((NZ,)),
             dma((NZ,)),
-            dma((3,)),
+            dma((2,)),
             dma((TILES + 1,)),
             dma((TILES + 1,)),
             dma((3,)),
@@ -660,7 +658,7 @@
         compiler_params=pltpu.CompilerParams(
             collective_id=0, has_side_effects=True, vmem_limit_bytes=56 * 1024 * 1024
         ),
-    )(hidden[0], frozen_weight, final_norm_gain[None, :], down_maps, up_maps, tenant, adapter)
+    )(hidden[0], frozen_weight, final_norm_gain, down_maps, up_maps, tenant, adapter)
     return gin[None], gup[None], gdown[None], loss
 
 

time: 145 us -> 134 us (0.924)
  the two profiles are of different devices: /device:TPU:6 before, /device:TPU:18 now
where the time goes in v2:
time: 134 us; the launch traced here: 133 us
  Pallas kernels  129 us (96%)
  local copies, waits for them, and re-layouts  2.65 us (2%)
    pallas_call x1, Pallas kernels, body(): pl.pallas_call(kernel, name='whole_step', out_shape=(pltpu.VMEM((TOK, HAL...  129 us

profile of v2, /device:TPU:18, one launch (start us, length us, event | category | flops | bytes accessed | tf_op | source)
XLA Modules:
  0.0 133.3 jit_solution(8373028722763959171)
XLA Ops:
  1.3 129.4 %whole_step.1 = (bf16[128,1792]{1,0:T(8,128)(2,1)S(1)}, f32[32,1792]{1,0:T(8,128)S(1)}, f32[32,1792]{1,0:T(8,128)S(1)}, f32[1,8]{1,0:T(1,128)S(1)}) custom-call(bf16[128,1792]{1,0:T(8,128)(2,1)} %bitcast.7, bf16[112,1792]{1,0:T(8,128)(2,1)} %w_hbm.1, f32[1792]{0:T(1024)} %gain_hbm.1, bf16[8,32,1792]{2,1,0:T(8,128)(2,1)} %down_hbm.1, ...), custom_call_target="tpu_custom_call" | custom-call | tf_op jit(solution)/shard_map/whole_step/pallas_call | solution.py:590
  130.7 0.8 copy.15
  131.4 0.7 copy.16
  132.1 0.5 copy.18
  132.6 0.7 copy.17

commit v3 on v2

--- a/solution.py
+++ b/solution.py
@@ -23,6 +23,7 @@
 OWNERS = 14
 TILE = 256
 TILES = 7
+LAG = 4
 
 logit_divisor = 0.05
 loss_scale = 256.0
@@ -76,6 +77,7 @@
     acc,
     x_own,
     x3,
+    x_pass,
     downs,
     ups,
     low_snd,
@@ -90,8 +92,9 @@
     s_rcv,
     s_all,
     mask_ref,
-    sum_snd,
-    sum_rcv,
+    gained_ref,
+    t_snd,
+    t_rcv,
     go,
     gl_snd,
     gl_rcv,
@@ -118,6 +121,7 @@
     gin_sem,
     rs_sem,
     ag_sem,
+    agz_sem,
 ):
     dp = lax.axis_index("dp")
     pipe = lax.axis_index("pipe")
@@ -134,6 +138,8 @@
     x_left = (pipe + 6) % 8
     partner = pipe + 1 - 2 * core
     peer = 1 - tensor
+    plus = {"dp": dp_y, "tensor": (tensor + y) % 2}
+    minus = {"dp": dp_y, "tensor": (tensor + 1 - y) % 2}
     before = (pipe + 7) % 8
     after = (pipe + 1) % 8
 
@@ -159,9 +165,10 @@
         {"pipe": before},
         {"pipe": after},
         {"tensor": peer},
+        {"dp": dp_y, "tensor": peer},
     ):
         pl.semaphore_signal(barrier, inc=1, device_id=where, device_id_type=MESH)
-    pl.semaphore_wait(barrier, 8)
+    pl.semaphore_wait(barrier, 9)
 
     def remote(src, dst, send, recv, where):
         copy = pltpu.make_async_remote_copy(
@@ -177,7 +184,7 @@
     def piece(zz, q, first, count):
         return wbuf.at[pl.ds(pl.multiple_of((zz * 2 + q) * SHARD + first, 16), count), columns]
 
-    chunks = ((0, CUT_A), (CUT_A, SHARD - CUT_A))
+    chunks = ((CUT_B, SHARD - CUT_B), (0, CUT_A), (CUT_A, CUT_B - CUT_A))
 
     @pl.when(x % 2 == 0)
     def _():
@@ -211,14 +218,11 @@
         )
 
     def share(zz, rel, number):
-        if number == 0:
-            part = piece(zz, own_q, 0, CUT_A)
-            remote(part, part, w_send.at[2], xy_sem.at[rel], {"pipe": x_right})
-        else:
-            part = piece(zz, own_q, CUT_A, CUT_B - CUT_A)
-            remote(part, part, w_send.at[3], xy_sem.at[rel], {"pipe": x_left})
-            part = piece(zz, own_q, CUT_B, SHARD - CUT_B)
-            remote(part, part, w_send.at[4], xy_sem.at[rel], {"dp": dp_y})
+        first, count = chunks[number]
+        part = piece(zz, own_q, first, count)
+        where = ({"dp": dp_y}, {"pipe": x_right}, {"pipe": x_left})[number]
+        remote(part, part, w_send.at[2 + number], xy_sem.at[rel], where)
+        if number == 2:
             part = piece(zz, own_q, 0, SHARD)
             remote(part, part, w_send.at[5], d2d_sem.at[0, rel], {"pipe": partner})
 
@@ -253,8 +257,8 @@
         gain_copy.wait()
         for number in range(8):
             x3[tensor * 8 + number] = x_own[:, number * PLANE : (number + 1) * PLANE]
-        mine = x3.at[pl.ds(tensor * 8, 8)]
-        remote(mine, mine, x_sem.at[0], x_sem.at[1], {"tensor": peer})
+        remote(x3.at[pl.ds(tensor * 8, 4)], x_pass.at[0], x_sem.at[0], x_sem.at[1], plus)
+        remote(x3.at[pl.ds(tensor * 8 + 4, 4)], x_pass.at[1], x_sem.at[0], x_sem.at[2], minus)
         picked = adapter_ref[0]
         low_snd[...] = nt(downs[picked], x_own[...])
         remote(low_snd, low_rcv, small_sem.at[0], small_sem.at[1], {"tensor": peer})
@@ -264,8 +268,17 @@
         column = lax.broadcasted_iota(jnp.int32, (ALL, ALL), 1)
         mask_ref[...] = jnp.where((tenants == own) & (row != column), 1.0, 0.0)
 
+    def pass_on():
+        arrived(x_pass.at[0], x_sem.at[1])
+        half = (tensor + 1 - y) % 2
+        remote(x_pass.at[0], x3.at[pl.ds(half * 8, 4)], x_sem.at[3], x_sem.at[4], plus)
+        arrived(x_pass.at[1], x_sem.at[2])
+        half = (tensor + y) % 2
+        remote(x_pass.at[1], x3.at[pl.ds(half * 8 + 4, 4)], x_sem.at[3], x_sem.at[5], minus)
+
     def first_terms():
-        arrived(x3.at[pl.ds(peer * 8, 8)], x_sem.at[1])
+        arrived(x3.at[pl.ds(peer * 8, 4)], x_sem.at[4])
+        arrived(x3.at[pl.ds(peer * 8 + 4, 4)], x_sem.at[5])
         arrived(low_rcv, small_sem.at[1])
         picked = adapter_ref[0]
         lowt[...] = (low_snd[...] + low_rcv[...]).astype(BF16)
@@ -278,13 +291,13 @@
         zr = right_z(k)
         zl = left_z(k)
 
-        for number in range(2):
+        for number in range(3):
 
             @pl.when(k <= 8)
             def _():
                 got(zr, rel, number)
 
-            @pl.when(k <= 7 - number)
+            @pl.when(k <= (7 if number < 2 else 6))
             def _():
                 forward(zr, rel, number, True)
 
@@ -296,7 +309,7 @@
             def _():
                 got(zl, k, number)
 
-            @pl.when((k >= 1) & (k <= 6 + number))
+            @pl.when((k >= 1) & (k <= (6 if number < 2 else 7)))
             def _():
                 forward(zl, k, number, False)
 
@@ -312,29 +325,33 @@
         def _():
             prepare()
 
-        @pl.when((k >= 1) & (k <= 9))
-        def _():
-            complement(right_z(k - 1), (NZ + 1 - k) % NZ)
-
-        @pl.when((k >= 2) & (k <= 8))
-        def _():
-            complement(left_z(k - 1), k - 1)
-
         @pl.when(k == 2)
         def _():
+            pass_on()
+
+        @pl.when(k == LAG)
+        def _():
             first_terms()
 
-        @pl.when(k >= 2)
-        def _():
-            compute(right_z(k - 2), (NZ + 2 - k) % NZ)
+        @pl.when(k >= LAG)
+        def _():
+            compute(right_z(k - LAG), (NZ + LAG - k) % NZ)
+
+        @pl.when((k >= LAG + 1) & (k <= LAG + 7))
+        def _():
+            compute(left_z(k - LAG), k - LAG)
+
+        @pl.when((k >= 2) & (k <= 10))
+        def _():
+            complement(right_z(k - 2), (NZ + 2 - k) % NZ)
 
         @pl.when((k >= 3) & (k <= 9))
         def _():
-            compute(left_z(k - 2), k - 2)
+            complement(left_z(k - 2), k - 2)
 
         return carry
 
-    lax.fori_loop(0, 11, step, 0)
+    lax.fori_loop(0, LAG + 9, step, 0)
 
     picked = adapter_ref[0]
 
@@ -364,10 +381,16 @@
         part = row_of(rel, y)
         remote(part, part, e_send.at[1], ey_sem.at[rel], {"dp": dp_y})
 
+    def e_send_diagonal(hops):
+        part = row_of(8, y)
+        remote(
+            part, part, e_send.at[0], ey_sem.at[8 - hops], {"dp": (dp_y + 32 + 2 * hops) % 32}
+        )
+
     for hops in (4, -4, 1, -1, 2, -2):
         e_send_z(0, hops)
     e_send_y(0)
-    second = jnp.sum(acc[...] * gain_ref[...] * per_token(pooled_ref[...]), axis=1, keepdims=True)
+    gained_ref[...] = (acc[...] * gain_ref[...]).astype(BF16)
     for rel in (15, 1, 14, 2, 12, 4, 11, 3, 13, 5, 10, 6, 8, 7, 9):
         arrived(row_of(rel, y), ez_sem.at[rel])
         if rel == 12:
@@ -381,7 +404,11 @@
             e_send_z(12, 2)
         if rel == 4:
             e_send_z(4, -2)
-        e_send_y(rel)
+        if rel == 8:
+            e_send_diagonal(1)
+            e_send_diagonal(-1)
+        if rel not in (7, 9):
+            e_send_y(rel)
 
     def e_last(rel, carry):
         arrived(e3.at[((z + rel) % NZ) * 2 + 1 - y], ey_sem.at[rel])
@@ -400,6 +427,8 @@
         jnp.sum(jnp.where(row == column, corner, 0.0), axis=0, keepdims=True), (8, TOK)
     )
     remote(s_snd, s_rcv, small_sem.at[4], small_sem.at[5], {"tensor": peer})
+    t_snd[...] = nt(gained_ref[...], e2[...]).astype(BF16)
+    remote(t_snd, t_rcv, small_sem.at[6], small_sem.at[7], {"tensor": peer})
     arrived(s_rcv, small_sem.at[5])
     block = s_snd[0:TOK, :] + s_rcv[0:TOK, :]
     both = s_snd[TOK:ALL, :] + s_rcv[TOK:ALL, :]
@@ -436,26 +465,17 @@
     loss_ref[...] = jnp.transpose(loss)[0:1, :]
     both = jnp.where(allowed, jnp.exp(own_scores - total) + jnp.exp(own_scores - total_row), 0.0)
     weights = loss_scale * (both - jnp.where(mated, 2.0, 0.0))
-    grad_emb = nn((weights * inverse_row).astype(BF16), e2[...]) / logit_divisor
-
+    rounded = (weights * inverse_row).astype(BF16)
+    grad_emb = nn(rounded, e2[...]) / logit_divisor
+    rounded = rounded.astype(F32) / logit_divisor
     unit = pooled_ref[...] * inverse
-    along_part = jnp.sum(unit * grad_emb, axis=1, keepdims=True)
-    gained = acc[...] * gain_ref[...]
-    first = jnp.sum(gained * per_token(grad_emb), axis=1, keepdims=True)
-    along_tokens = per_token(jnp.broadcast_to(along_part, (ROWS, TOK)))[:, 0:1]
-    sum_snd[...] = as_lanes((first, second, along_tokens))
-    remote(sum_snd, sum_rcv, small_sem.at[6], small_sem.at[7], {"tensor": peer})
-    arrived(sum_rcv, small_sem.at[7])
-    sums = as_columns(sum_snd[...] + sum_rcv[...])
-    first_sum, second_sum, along = sums[:, 0:1], sums[:, 1:2], sums[:, 2:3]
+    along = inverse * jnp.sum(rounded * own_raw, axis=1, keepdims=True)
+    factors = rounded - jnp.where(own_row == own_column, along * inverse, 0.0)
+    arrived(t_rcv, small_sem.at[7])
+    meets = t_snd[...].astype(F32) + t_rcv[...].astype(F32)
     inverse_tokens = per_token(jnp.broadcast_to(inverse, (ROWS, TOK)))[:, 0:1]
-    inner = inverse_tokens * (first_sum - along * inverse_tokens * second_sum) * (1.0 / SEQ)
-    spread = (
-        inverse_tokens
-        * (per_token(grad_emb) - per_token(unit) * along)
-        * gain_ref[...]
-        * (1.0 / SEQ)
-    )
+    inner = inverse_tokens * jnp.sum(per_token(factors) * meets, axis=1, keepdims=True) * (1.0 / SEQ)
+    spread = per_token(inverse * (grad_emb - unit * along) * gain_ref[...] * (1.0 / SEQ))
     pull = inner * token_inv * token_inv * (1.0 / WIDTH)
     go[...] = (token_inv * (spread - acc[...] * pull)).astype(BF16)
 
@@ -463,6 +483,10 @@
     remote(gl_snd, gl_rcv, small_sem.at[8], small_sem.at[9], {"tensor": peer})
 
     owner = z < OWNERS
+
+    def far_first(number):
+        away = 8 - (number + 1) // 2
+        return (number % 2) * away + (1 - number % 2) * (NZ - away)
 
     def scatter(buffer, values, kind):
         for number in range(OWNERS):
@@ -472,8 +496,8 @@
         def _():
             rs_rcv[dp] = buffer[jnp.minimum(z, OWNERS - 1)]
 
-        def one(off, carry):
-            zz = (z + off) % NZ
+        def one(number, carry):
+            zz = (z + far_first(number)) % NZ
             there = zz * 2 + kind
 
             @pl.when((zz < OWNERS) & (there != dp))
@@ -494,13 +518,11 @@
         remote(part_snd.at[j], part_rcv.at[j], part_sem.at[TILES], part_sem.at[j], {"tensor": peer})
         return carry
 
-    lax.fori_loop(0, 3, part_step, 0)
-
     arrived(gl_rcv, small_sem.at[9])
     glt[...] = (gl_snd[...] + gl_rcv[...]).astype(BF16)
     scatter(rs_down, nn(glt[...], x_own[...]), 1)
 
-    lax.fori_loop(3, TILES, part_step, 0)
+    lax.fori_loop(0, TILES, part_step, 0)
 
     def own_step(j, carry):
         rows = pl.ds(pl.multiple_of(tensor * HALF + j * TILE, TILE), TILE)
@@ -516,11 +538,15 @@
         mine = ag.at[y * OWNERS + jnp.minimum(z, OWNERS - 1)]
         mine[...] = jnp.sum(rs_rcv[...].astype(F32), axis=0).astype(BF16)
 
-        def one(off, carry):
-            remote(mine, mine, ag_sem.at[0], ag_sem.at[1], {"dp": (dp + off) % 32})
+        def one(number, carry):
+            off = far_first(number)
+            remote(
+                mine, mine, ag_sem.at[0], agz_sem.at[NZ - off], {"dp": ((z + off) % NZ) * 2 + y}
+            )
             return carry
 
-        lax.fori_loop(1, 32, one, 0)
+        remote(mine, mine, ag_sem.at[1], ag_sem.at[2], {"dp": dp_y})
+        lax.fori_loop(0, NZ - 1, one, 0)
 
     def gin_step(j, carry):
         at = pl.ds(pl.multiple_of(j * TILE, TILE), TILE)
@@ -531,20 +557,27 @@
 
     lax.fori_loop(0, TILES, gin_step, 0)
 
-    @pl.when(owner)
-    def _():
-        arrived(ag.at[pl.ds(0, 2 * OWNERS - 1)], ag_sem.at[1])
-
-    @pl.when(z >= OWNERS)
-    def _():
-        arrived(ag, ag_sem.at[1])
+    def ag_step(number, carry):
+        rel = far_first(NZ - 2 - number)
+        zz = (z + rel) % NZ
+
+        @pl.when(zz < OWNERS)
+        def _():
+            part = ag.at[y * OWNERS + zz]
+            arrived(part, agz_sem.at[rel])
+            remote(part, part, ag_sem.at[1], ag_sem.at[2], {"dp": dp_y})
+
+        return carry
+
+    lax.fori_loop(0, NZ - 1, ag_step, 0)
+    arrived(ag.at[pl.ds((1 - y) * OWNERS, OWNERS)], ag_sem.at[2])
 
     for number in range(OWNERS):
         at = slice(number * 128, (number + 1) * 128)
         gup_ref[:, at] = ag[number].astype(F32)
         gdown_ref[:, at] = ag[OWNERS + number].astype(F32)
 
-    for number, rows in enumerate((7 * SHARD + CUT_A, 8 * SHARD - CUT_A, NZ * 48, NZ * 48, NZ * 16, 2 * NZ * SHARD)):
+    for number, rows in enumerate((7 * SHARD + 64, 7 * SHARD + 48, NZ * 16, NZ * 48, NZ * 48, 2 * NZ * SHARD)):
         arrived(wbuf.at[pl.ds(0, rows), pl.ds(0, CORE)], w_send.at[number])
 
     @pl.when(x % 2 == 1)
@@ -552,12 +585,13 @@
         arrived(wbuf.at[pl.ds(0, SHARD), pl.ds(0, CORE)], w_send.at[6])
 
     arrived(x3.at[pl.ds(0, 8)], x_sem.at[0])
+    arrived(x3.at[pl.ds(0, 8)], x_sem.at[3])
     arrived(low_snd, small_sem.at[0])
     arrived(tok_snd, small_sem.at[2])
-    arrived(e3.at[pl.ds(0, 15)], e_send.at[0])
-    arrived(e3.at[pl.ds(0, 16)], e_send.at[1])
+    arrived(e3.at[pl.ds(0, 17)], e_send.at[0])
+    arrived(e3.at[pl.ds(0, 14)], e_send.at[1])
     arrived(s_snd, small_sem.at[4])
-    arrived(sum_snd, small_sem.at[6])
+    arrived(t_snd, small_sem.at[6])
     arrived(gl_snd, small_sem.at[8])
     arrived(part_snd, part_sem.at[TILES])
     arrived(gin_snd, gin_sem.at[TILES])
@@ -573,7 +607,9 @@
 
     @pl.when(owner)
     def _():
-        arrived(rs_rcv.at[pl.ds(0, 31)], ag_sem.at[0])
+        arrived(rs_rcv.at[pl.ds(0, NZ - 1)], ag_sem.at[0])
+
+    arrived(rs_up, ag_sem.at[1])
 
     def gin_last(j, carry):
         at = pl.ds(pl.multiple_of(j * TILE, TILE), TILE)
@@ -612,6 +648,7 @@
             pltpu.VMEM((TOK, HALF), F32),
             pltpu.VMEM((TOK, HALF), BF16),
             pltpu.VMEM((NZ, TOK, PLANE), BF16),
+            pltpu.VMEM((2, 4, TOK, PLANE), BF16),
             pltpu.VMEM((8, RANK, HALF), BF16),
             pltpu.VMEM((8, RANK, HALF), BF16),
             pltpu.VMEM((RANK, TOK), F32),
@@ -626,8 +663,9 @@
             pltpu.VMEM((ALL + 8, TOK), F32),
             pltpu.VMEM((ALL, ALL), F32),
             pltpu.VMEM((ALL, ALL), F32),
-            pltpu.VMEM((8, TOK), F32),
-            pltpu.VMEM((8, TOK), F32),
+            pltpu.VMEM((TOK, HALF), BF16),
+            pltpu.VMEM((TOK, ALL), BF16),
+            pltpu.VMEM((TOK, ALL), BF16),
             pltpu.VMEM((TOK, HALF), BF16),
             pltpu.VMEM((RANK, TOK), F32),
             pltpu.VMEM((RANK, TOK), F32),
@@ -641,11 +679,11 @@
             pltpu.VMEM((32, RANK, 128), BF16),
             pltpu.VMEM((2 * OWNERS, RANK, 128), BF16),
             dma((4,)),
-            dma((NZ, 2)),
+            dma((NZ, 3)),
             dma((NZ,)),
             dma((2, NZ)),
             dma((7,)),
-            dma((2,)),
+            dma((6,)),
             dma((10,)),
             dma((NZ,)),
             dma((NZ,)),
@@ -653,7 +691,8 @@
             dma((TILES + 1,)),
             dma((TILES + 1,)),
             dma((3,)),
-            dma((2,)),
+            dma((3,)),
+            dma((NZ,)),
         ],
         compiler_params=pltpu.CompilerParams(
             collective_id=0, has_side_effects=True, vmem_limit_bytes=56 * 1024 * 1024

time: 134 us -> 119 us (0.89)
  the two profiles are of different devices: /device:TPU:18 before, /device:TPU:4 now
where the time goes in v3:
time: 119 us; the launch traced here: 118 us
  Pallas kernels  114 us (96%)
  local copies, waits for them, and re-layouts  2.65 us (2%)
  between operations  1.29 us (1%)
    pallas_call x1, Pallas kernels, body(): pl.pallas_call(kernel, name='whole_step', out_shape=(pltpu.VMEM((TOK, HAL...  114 us
    unnamed x4, local copies, waits for them, and re-layouts  2.65 us

profile of v3, /device:TPU:4, one launch (start us, length us, event | category | flops | bytes accessed | tf_op | source)
XLA Modules:
  0.0 118.3 jit_solution(17704570187698912641)
XLA Ops:
  1.3 114.4 %whole_step.1 = (bf16[128,1792]{1,0:T(8,128)(2,1)S(1)}, f32[32,1792]{1,0:T(8,128)S(1)}, f32[32,1792]{1,0:T(8,128)S(1)}, f32[1,8]{1,0:T(1,128)S(1)}) custom-call(bf16[128,1792]{1,0:T(8,128)(2,1)} %bitcast.7, bf16[112,1792]{1,0:T(8,128)(2,1)} %w_hbm.1, f32[1792]{0:T(1024)} %gain_hbm.1, bf16[8,32,1792]{2,1,0:T(8,128)(2,1)} %down_hbm.1, ...), custom_call_target="tpu_custom_call" | custom-call | tf_op jit(solution)/shard_map/whole_step/pallas_call | solution.py:626
  115.7 0.8 copy.15
  116.4 0.7 copy.16
  117.1 0.5 copy.18
  117.6 0.7 copy.17

commit v4 on v3

--- a/solution.py
+++ b/solution.py
@@ -369,45 +369,42 @@
     def row_of(rel, yy):
         return e3.at[((z + rel) % NZ) * 2 + yy]
 
-    def e_send_z(rel, hops, half=None):
+    def e_send_z(rel, hops, half=None, across=False):
         part = row_of(rel, y)
         if half is not None:
             part = part.at[:, pl.ds(half * CORE, CORE)]
+        there = (rel - hops) % NZ
+        to = dp_y if across else dp
         remote(
-            part, part, e_send.at[0], ez_sem.at[(rel - hops) % NZ], {"dp": (dp + 32 + 2 * hops) % 32}
+            part,
+            part,
+            e_send.at[0],
+            ey_sem.at[there] if across else ez_sem.at[there],
+            {"dp": (to + 32 + 2 * hops) % 32},
         )
 
     def e_send_y(rel):
         part = row_of(rel, y)
         remote(part, part, e_send.at[1], ey_sem.at[rel], {"dp": dp_y})
 
-    def e_send_diagonal(hops):
-        part = row_of(8, y)
-        remote(
-            part, part, e_send.at[0], ey_sem.at[8 - hops], {"dp": (dp_y + 32 + 2 * hops) % 32}
-        )
-
-    for hops in (4, -4, 1, -1, 2, -2):
+    for hops in (6, -6, 3, -3, 1, -1):
         e_send_z(0, hops)
     e_send_y(0)
     gained_ref[...] = (acc[...] * gain_ref[...]).astype(BF16)
-    for rel in (15, 1, 14, 2, 12, 4, 11, 3, 13, 5, 10, 6, 8, 7, 9):
+    for rel in (15, 1, 13, 3, 10, 6, 14, 2, 12, 4, 11, 5, 9, 7, 8):
         arrived(row_of(rel, y), ez_sem.at[rel])
-        if rel == 12:
-            e_send_z(12, 4, 0)
-        if rel == 4:
-            e_send_z(4, -4, 1)
-        if rel % 4 == 0:
-            e_send_z(rel, 1)
-            e_send_z(rel, -1)
-        if rel == 12:
-            e_send_z(12, 2)
-        if rel == 4:
-            e_send_z(4, -2)
-        if rel == 8:
-            e_send_diagonal(1)
-            e_send_diagonal(-1)
-        if rel not in (7, 9):
+        if rel in (3, 13):
+            for hops in (1, -1):
+                e_send_z(rel, hops)
+        if rel in (6, 10):
+            for across in (True, False):
+                for hops in (1, -1):
+                    e_send_z(rel, hops, across=across)
+                if rel == 6:
+                    e_send_z(6, -2, 0, across)
+                else:
+                    e_send_z(10, 2, 1, across)
+        if rel not in (5, 7, 8, 9, 11):
             e_send_y(rel)
 
     def e_last(rel, carry):
@@ -518,11 +515,13 @@
         remote(part_snd.at[j], part_rcv.at[j], part_sem.at[TILES], part_sem.at[j], {"tensor": peer})
         return carry
 
+    lax.fori_loop(0, 2, part_step, 0)
+
     arrived(gl_rcv, small_sem.at[9])
     glt[...] = (gl_snd[...] + gl_rcv[...]).astype(BF16)
     scatter(rs_down, nn(glt[...], x_own[...]), 1)
 
-    lax.fori_loop(0, TILES, part_step, 0)
+    lax.fori_loop(2, TILES, part_step, 0)
 
     def own_step(j, carry):
         rows = pl.ds(pl.multiple_of(tensor * HALF + j * TILE, TILE), TILE)
@@ -588,8 +587,8 @@
     arrived(x3.at[pl.ds(0, 8)], x_sem.at[3])
     arrived(low_snd, small_sem.at[0])
     arrived(tok_snd, small_sem.at[2])
-    arrived(e3.at[pl.ds(0, 17)], e_send.at[0])
-    arrived(e3.at[pl.ds(0, 14)], e_send.at[1])
+    arrived(e3.at[pl.ds(0, 20)], e_send.at[0])
+    arrived(e3.at[pl.ds(0, 11)], e_send.at[1])
     arrived(s_snd, small_sem.at[4])
     arrived(t_snd, small_sem.at[6])
     arrived(gl_snd, small_sem.at[8])
@@ -617,6 +616,19 @@
         return carry
 
     lax.fori_loop(0, TILES, gin_last, 0)
+
+
+def put_out(gin, gup, gdown, loss, gin_hbm, gup_hbm, gdown_hbm, loss_hbm, sems):
+    copies = [
+        pltpu.make_async_copy(src, dst, sems.at[number])
+        for number, (src, dst) in enumerate(
+            ((gin, gin_hbm), (gup, gup_hbm), (gdown, gdown_hbm), (loss, loss_hbm))
+        )
+    ]
+    for copy in copies:
+        copy.start()
+    for copy in copies:
+        copy.wait()
 
 
 def body(hidden, frozen_weight, final_norm_gain, down_maps, up_maps, tenant, adapter):
@@ -698,6 +710,20 @@
             collective_id=0, has_side_effects=True, vmem_limit_bytes=56 * 1024 * 1024
         ),
     )(hidden[0], frozen_weight, final_norm_gain, down_maps, up_maps, tenant, adapter)
+    gin, gup, gdown, loss = pl.pallas_call(
+        put_out,
+        name="put_out",
+        out_shape=(
+            jax.ShapeDtypeStruct((TOK, HALF), BF16),
+            jax.ShapeDtypeStruct((RANK, HALF), F32),
+            jax.ShapeDtypeStruct((RANK, HALF), F32),
+            jax.ShapeDtypeStruct((1, ROWS), F32),
+        ),
+        in_specs=[vmem] * 4,
+        out_specs=(anywhere,) * 4,
+        scratch_shapes=[dma((4,))],
+        compiler_params=pltpu.CompilerParams(vmem_limit_bytes=4 * 1024 * 1024),
+    )(gin, gup, gdown, loss)
     return gin[None], gup[None], gdown[None], loss
 
 

time: 119 us -> 120 us (level)
  Pallas kernels: 114 us -> 119 us
  local copies, waits for them, and re-layouts: 2.65 us -> 0 us
    pallas_call x1, Pallas kernels: 114 us -> 118 us  [body(): pl.pallas_call(kernel, name='whole_step', out_shape=(pltpu.VMEM((TOK, HAL...]
    unnamed x4 -> x0, local copies, waits for them, and re-layouts: 2.65 us -> none
where the time goes in v4:
time: 120 us
  Pallas kernels  119 us (99%)
  between operations  1.29 us (1%)
    pallas_call x1, Pallas kernels, body(): pl.pallas_call(kernel, name='whole_step', out_shape=(pltpu.VMEM((TOK, HAL...  118 us

profile of v4, /device:TPU:4, one launch (start us, length us, event | category | flops | bytes accessed | tf_op | source)
XLA Modules:
  0.0 120.3 jit_solution(2678099740447417119)
XLA Ops:
  1.3 118.0 %whole_step.1 = (bf16[128,1792]{1,0:T(8,128)(2,1)S(1)}, f32[32,1792]{1,0:T(8,128)S(1)}, f32[32,1792]{1,0:T(8,128)S(1)}, f32[1,8]{1,0:T(1,128)S(1)}) custom-call(bf16[128,1792]{1,0:T(8,128)(2,1)} %bitcast.4, bf16[112,1792]{1,0:T(8,128)(2,1)} %w_hbm.1, f32[1792]{0:T(1024)} %gain_hbm.1, bf16[8,32,1792]{2,1,0:T(8,128)(2,1)} %down_hbm.1, ...), custom_call_target="tpu_custom_call" | custom-call | tf_op jit(solution)/shard_map/whole_step/pallas_call | solution.py:638
  119.3 1.0 put_out.1

commit v5 on v3

--- a/solution.py
+++ b/solution.py
@@ -23,6 +23,7 @@
 OWNERS = 14
 TILE = 256
 TILES = 7
+FAR = 7
 LAG = 4
 
 logit_divisor = 0.05
@@ -122,6 +123,7 @@
     rs_sem,
     ag_sem,
     agz_sem,
+    ags_sem,
 ):
     dp = lax.axis_index("dp")
     pipe = lax.axis_index("pipe")
@@ -410,12 +412,11 @@
         if rel not in (7, 9):
             e_send_y(rel)
 
-    def e_last(rel, carry):
-        arrived(e3.at[((z + rel) % NZ) * 2 + 1 - y], ey_sem.at[rel])
-        return carry
-
-    lax.fori_loop(0, NZ, e_last, 0)
-    e2[...] = e3[...].astype(F32).reshape(ALL, HALF).astype(BF16)
+    for rel in (0, 15, 1, 14, 2, 12, 4, 11, 3, 13, 5, 10, 6, 8, 7, 9):
+        zz = (z + rel) % NZ
+        arrived(row_of(rel, 1 - y), ey_sem.at[rel])
+        plane = e3[pl.ds(zz * 2, 2)].astype(F32).reshape(2 * ROWS, HALF).astype(BF16)
+        e2[pl.ds(pl.multiple_of(zz * 2 * ROWS, 2 * ROWS), 2 * ROWS), :] = plane
 
     row = lax.broadcasted_iota(jnp.int32, (TOK, TOK), 0)
     column = lax.broadcasted_iota(jnp.int32, (TOK, TOK), 1)
@@ -540,12 +541,18 @@
 
         def one(number, carry):
             off = far_first(number)
-            remote(
-                mine, mine, ag_sem.at[0], agz_sem.at[NZ - off], {"dp": ((z + off) % NZ) * 2 + y}
-            )
+            there = ((z + off) % NZ) * 2
+            remote(mine, mine, ag_sem.at[0], agz_sem.at[NZ - off], {"dp": there + y})
+
+            @pl.when(number >= FAR)
+            def _():
+                remote(
+                    mine, mine, ag_sem.at[0], agz_sem.at[2 * NZ - off], {"dp": there + 1 - y}
+                )
+
             return carry
 
-        remote(mine, mine, ag_sem.at[1], ag_sem.at[2], {"dp": dp_y})
+        remote(mine, mine, ags_sem.at[0], agz_sem.at[NZ], {"dp": dp_y})
         lax.fori_loop(0, NZ - 1, one, 0)
 
     def gin_step(j, carry):
@@ -558,19 +565,32 @@
     lax.fori_loop(0, TILES, gin_step, 0)
 
     def ag_step(number, carry):
-        rel = far_first(NZ - 2 - number)
+        rel = far_first(number)
         zz = (z + rel) % NZ
 
         @pl.when(zz < OWNERS)
         def _():
             part = ag.at[y * OWNERS + zz]
             arrived(part, agz_sem.at[rel])
-            remote(part, part, ag_sem.at[1], ag_sem.at[2], {"dp": dp_y})
+
+            @pl.when(number < FAR)
+            def _():
+                remote(part, part, ags_sem.at[rel], agz_sem.at[NZ + rel], {"dp": dp_y})
 
         return carry
 
     lax.fori_loop(0, NZ - 1, ag_step, 0)
-    arrived(ag.at[pl.ds((1 - y) * OWNERS, OWNERS)], ag_sem.at[2])
+
+    def ag_last(rel, carry):
+        zz = (z + rel) % NZ
+
+        @pl.when(zz < OWNERS)
+        def _():
+            arrived(ag.at[(1 - y) * OWNERS + zz], agz_sem.at[NZ + rel])
+
+        return carry
+
+    lax.fori_loop(0, NZ, ag_last, 0)
 
     for number in range(OWNERS):
         at = slice(number * 128, (number + 1) * 128)
@@ -607,9 +627,19 @@
 
     @pl.when(owner)
     def _():
-        arrived(rs_rcv.at[pl.ds(0, NZ - 1)], ag_sem.at[0])
-
-    arrived(rs_up, ag_sem.at[1])
+        arrived(rs_rcv.at[pl.ds(0, 2 * (NZ - 1) - FAR)], ag_sem.at[0])
+        arrived(ag.at[0], ags_sem.at[0])
+
+    def ag_left(number, carry):
+        rel = far_first(number)
+
+        @pl.when((z + rel) % NZ < OWNERS)
+        def _():
+            arrived(ag.at[0], ags_sem.at[rel])
+
+        return carry
+
+    lax.fori_loop(0, FAR, ag_left, 0)
 
     def gin_last(j, carry):
         at = pl.ds(pl.multiple_of(j * TILE, TILE), TILE)
@@ -617,6 +647,19 @@
         return carry
 
     lax.fori_loop(0, TILES, gin_last, 0)
+
+
+def put_out(gin, gup, gdown, loss, gin_hbm, gup_hbm, gdown_hbm, loss_hbm, sems):
+    copies = [
+        pltpu.make_async_copy(src, dst, sems.at[number])
+        for number, (src, dst) in enumerate(
+            ((gin, gin_hbm), (gup, gup_hbm), (gdown, gdown_hbm), (loss, loss_hbm))
+        )
+    ]
+    for copy in copies:
+        copy.start()
+    for copy in copies:
+        copy.wait()
 
 
 def body(hidden, frozen_weight, final_norm_gain, down_maps, up_maps, tenant, adapter):
@@ -691,13 +734,28 @@
             dma((TILES + 1,)),
             dma((TILES + 1,)),
             dma((3,)),
-            dma((3,)),
+            dma((1,)),
+            dma((2 * NZ,)),
             dma((NZ,)),
         ],
         compiler_params=pltpu.CompilerParams(
             collective_id=0, has_side_effects=True, vmem_limit_bytes=56 * 1024 * 1024
         ),
     )(hidden[0], frozen_weight, final_norm_gain, down_maps, up_maps, tenant, adapter)
+    gin, gup, gdown, loss = pl.pallas_call(
+        put_out,
+        name="put_out",
+        out_shape=(
+            jax.ShapeDtypeStruct((TOK, HALF), BF16),
+            jax.ShapeDtypeStruct((RANK, HALF), F32),
+            jax.ShapeDtypeStruct((RANK, HALF), F32),
+            jax.ShapeDtypeStruct((1, ROWS), F32),
+        ),
+        in_specs=[vmem] * 4,
+        out_specs=(anywhere,) * 4,
+        scratch_shapes=[dma((4,))],
+        compiler_params=pltpu.CompilerParams(vmem_limit_bytes=4 * 1024 * 1024),
+    )(gin, gup, gdown, loss)
     return gin[None], gup[None], gdown[None], loss
 
 

time: 119 us -> 119 us (level)
  Pallas kernels: 114 us -> 117 us
  local copies, waits for them, and re-layouts: 2.65 us -> 0 us
    unnamed x4 -> x0, local copies, waits for them, and re-layouts: 2.65 us -> none
    pallas_call x1, Pallas kernels: 114 us -> 116 us  [body(): pl.pallas_call(kernel, name='whole_step', out_shape=(pltpu.VMEM((TOK, HAL...]
where the time goes in v5:
time: 119 us
  Pallas kernels  117 us (98%)
  between operations  1.29 us (1%)
    pallas_call x1, Pallas kernels, body(): pl.pallas_call(kernel, name='whole_step', out_shape=(pltpu.VMEM((TOK, HAL...  116 us

profile of v5, /device:TPU:4, one launch (start us, length us, event | category | flops | bytes accessed | tf_op | source)
XLA Modules:
  0.0 118.7 jit_solution(14827618205919974833)
XLA Ops:
  1.3 116.5 %whole_step.1 = (bf16[128,1792]{1,0:T(8,128)(2,1)S(1)}, f32[32,1792]{1,0:T(8,128)S(1)}, f32[32,1792]{1,0:T(8,128)S(1)}, f32[1,8]{1,0:T(1,128)S(1)}) custom-call(bf16[128,1792]{1,0:T(8,128)(2,1)} %bitcast.4, bf16[112,1792]{1,0:T(8,128)(2,1)} %w_hbm.1, f32[1792]{0:T(1024)} %gain_hbm.1, bf16[8,32,1792]{2,1,0:T(8,128)(2,1)} %down_hbm.1, ...), custom_call_target="tpu_custom_call" | custom-call | tf_op jit(solution)/shard_map/whole_step/pallas_call | solution.py:669
  117.7 1.0 put_out.1

commit v6 on v3

--- a/solution.py
+++ b/solution.py
@@ -23,7 +23,8 @@
 OWNERS = 14
 TILE = 256
 TILES = 7
-LAG = 4
+LAG = 5
+CATCH = 9
 
 logit_divisor = 0.05
 loss_scale = 256.0
@@ -333,13 +334,15 @@
         def _():
             first_terms()
 
-        @pl.when(k >= LAG)
-        def _():
-            compute(right_z(k - LAG), (NZ + LAG - k) % NZ)
-
-        @pl.when((k >= LAG + 1) & (k <= LAG + 7))
-        def _():
-            compute(left_z(k - LAG), k - LAG)
+        for lag, begin, end in ((LAG, LAG, CATCH), (LAG - 1, CATCH, LAG + 7)):
+
+            @pl.when((k >= begin) & (k <= end))
+            def _():
+                compute(right_z(k - lag), (NZ + lag - k) % NZ)
+
+            @pl.when((k >= begin) & (k <= end) & (k >= lag + 1) & (k <= lag + 7))
+            def _():
+                compute(left_z(k - lag), k - lag)
 
         @pl.when((k >= 2) & (k <= 10))
         def _():
@@ -351,7 +354,7 @@
 
         return carry
 
-    lax.fori_loop(0, LAG + 9, step, 0)
+    lax.fori_loop(0, LAG + 8, step, 0)
 
     picked = adapter_ref[0]
 
@@ -617,6 +620,19 @@
         return carry
 
     lax.fori_loop(0, TILES, gin_last, 0)
+
+
+def put_out(gin, gup, gdown, loss, gin_hbm, gup_hbm, gdown_hbm, loss_hbm, sems):
+    copies = [
+        pltpu.make_async_copy(src, dst, sems.at[number])
+        for number, (src, dst) in enumerate(
+            ((gin, gin_hbm), (gup, gup_hbm), (gdown, gdown_hbm), (loss, loss_hbm))
+        )
+    ]
+    for copy in copies:
+        copy.start()
+    for copy in copies:
+        copy.wait()
 
 
 def body(hidden, frozen_weight, final_norm_gain, down_maps, up_maps, tenant, adapter):
@@ -698,6 +714,20 @@
             collective_id=0, has_side_effects=True, vmem_limit_bytes=56 * 1024 * 1024
         ),
     )(hidden[0], frozen_weight, final_norm_gain, down_maps, up_maps, tenant, adapter)
+    gin, gup, gdown, loss = pl.pallas_call(
+        put_out,
+        name="put_out",
+        out_shape=(
+            jax.ShapeDtypeStruct((TOK, HALF), BF16),
+            jax.ShapeDtypeStruct((RANK, HALF), F32),
+            jax.ShapeDtypeStruct((RANK, HALF), F32),
+            jax.ShapeDtypeStruct((1, ROWS), F32),
+        ),
+        in_specs=[vmem] * 4,
+        out_specs=(anywhere,) * 4,
+        scratch_shapes=[dma((4,))],
+        compiler_params=pltpu.CompilerParams(vmem_limit_bytes=4 * 1024 * 1024),
+    )(gin, gup, gdown, loss)
     return gin[None], gup[None], gdown[None], loss
 
 

time: 119 us -> 118 us (level)
  Pallas kernels: 114 us -> 117 us
  local copies, waits for them, and re-layouts: 2.65 us -> 0 us
    unnamed x4 -> x0, local copies, waits for them, and re-layouts: 2.65 us -> none
    pallas_call x1, Pallas kernels: 114 us -> 116 us  [body(): pl.pallas_call(kernel, name='whole_step', out_shape=(pltpu.VMEM((TOK, HAL...]
where the time goes in v6:
time: 118 us
  Pallas kernels  117 us (99%)
  between operations  1.29 us (1%)
    pallas_call x1, Pallas kernels, body(): pl.pallas_call(kernel, name='whole_step', out_shape=(pltpu.VMEM((TOK, HAL...  116 us

profile of v6, /device:TPU:4, one launch (start us, length us, event | category | flops | bytes accessed | tf_op | source)
XLA Modules:
  0.0 118.0 jit_solution(13470652940851423717)
XLA Ops:
  1.3 115.8 %whole_step.1 = (bf16[128,1792]{1,0:T(8,128)(2,1)S(1)}, f32[32,1792]{1,0:T(8,128)S(1)}, f32[32,1792]{1,0:T(8,128)S(1)}, f32[1,8]{1,0:T(1,128)S(1)}) custom-call(bf16[128,1792]{1,0:T(8,128)(2,1)} %bitcast.4, bf16[112,1792]{1,0:T(8,128)(2,1)} %w_hbm.1, f32[1792]{0:T(1024)} %gain_hbm.1, bf16[8,32,1792]{2,1,0:T(8,128)(2,1)} %down_hbm.1, ...), custom_call_target="tpu_custom_call" | custom-call | tf_op jit(solution)/shard_map/whole_step/pallas_call | solution.py:642
  117.1 1.0 put_out.1

commit v7 on v6

--- a/solution.py
+++ b/solution.py
@@ -23,8 +23,7 @@
 OWNERS = 14
 TILE = 256
 TILES = 7
-LAG = 5
-CATCH = 9
+LAG = 4
 
 logit_divisor = 0.05
 loss_scale = 256.0
@@ -334,15 +333,13 @@
         def _():
             first_terms()
 
-        for lag, begin, end in ((LAG, LAG, CATCH), (LAG - 1, CATCH, LAG + 7)):
-
-            @pl.when((k >= begin) & (k <= end))
-            def _():
-                compute(right_z(k - lag), (NZ + lag - k) % NZ)
-
-            @pl.when((k >= begin) & (k <= end) & (k >= lag + 1) & (k <= lag + 7))
-            def _():
-                compute(left_z(k - lag), k - lag)
+        @pl.when(k >= LAG)
+        def _():
+            compute(right_z(k - LAG), (NZ + LAG - k) % NZ)
+
+        @pl.when((k >= LAG + 1) & (k <= LAG + 7))
+        def _():
+            compute(left_z(k - LAG), k - LAG)
 
         @pl.when((k >= 2) & (k <= 10))
         def _():
@@ -354,7 +351,7 @@
 
         return carry
 
-    lax.fori_loop(0, LAG + 8, step, 0)
+    lax.fori_loop(0, LAG + 9, step, 0)
 
     picked = adapter_ref[0]
 

time: 118 us -> 117 us (level)
  Pallas kernels: 117 us -> 115 us
    pallas_call x1, Pallas kernels: 116 us -> 114 us  [body(): pl.pallas_call(kernel, name='whole_step', out_shape=(pltpu.VMEM((TOK, HAL...]
where the time goes in v7:
time: 117 us
  Pallas kernels  115 us (98%)
  between operations  1.29 us (1%)
    pallas_call x1, Pallas kernels, body(): pl.pallas_call(kernel, name='whole_step', out_shape=(pltpu.VMEM((TOK, HAL...  114 us

profile of v7, /device:TPU:4, one launch (start us, length us, event | category | flops | bytes accessed | tf_op | source)
XLA Modules:
  0.0 116.6 jit_solution(14794977881934874350)
XLA Ops:
  1.3 114.4 %whole_step.1 = (bf16[128,1792]{1,0:T(8,128)(2,1)S(1)}, f32[32,1792]{1,0:T(8,128)S(1)}, f32[32,1792]{1,0:T(8,128)S(1)}, f32[1,8]{1,0:T(1,128)S(1)}) custom-call(bf16[128,1792]{1,0:T(8,128)(2,1)} %bitcast.4, bf16[112,1792]{1,0:T(8,128)(2,1)} %w_hbm.1, f32[1792]{0:T(1024)} %gain_hbm.1, bf16[8,32,1792]{2,1,0:T(8,128)(2,1)} %down_hbm.1, ...), custom_call_target="tpu_custom_call" | custom-call | tf_op jit(solution)/shard_map/whole_step/pallas_call | solution.py:639
  115.7 1.0 put_out.1
